TPU v7x, 32 devices: a 4x2x2 block of a 4x4x8 slice. The times are simulated.
32 devices in a mesh: dp: 4 (over y, z), tp: 8 (over x, core).
Axes of the slice: x: 4, y: 2, z: 2, core: 2. Of those that a mesh axis runs over, the one named last changes fastest.
The devices are a block of a 4x4x8 slice.
Arguments:
- x_seq: bfloat16 [3, 512, 4096], P(None, 'dp'), parts along dimension 1
- cache_len: int32 [512], P('dp'), parts along dimension 0
- k_cache: bfloat16 [512, 8, 256, 128], P('dp', 'tp'), parts along dimension 0
- v_cache: bfloat16 [512, 8, 256, 128], P('dp', 'tp'), parts along dimension 0
- w_q: bfloat16 [4096, 4096], P(None, 'tp')
- w_k: bfloat16 [4096, 1024], P(None, 'tp')
- w_v: bfloat16 [4096, 1024], P(None, 'tp')
- w_o: bfloat16 [4096, 4096], P('tp')
- w_gate: bfloat16 [4096, 14336], P(None, 'tp')
- w_up: bfloat16 [4096, 14336], P(None, 'tp')
- w_down: bfloat16 [14336, 4096], P('tp')
- g_q: bfloat16 [4096], P('tp')
- g_k: bfloat16 [1024], P('tp')
- g_attn: bfloat16 [4096], replicated
- g_mlp: bfloat16 [4096], replicated
Outputs:
- output 1: bfloat16 [3, 512, 4096], P(None, 'dp'), parts along dimension 1
- output 2: bfloat16 [512, 8, 256, 128], P('dp', 'tp'), parts along dimension 0
- output 3: bfloat16 [512, 8, 256, 128], P('dp', 'tp'), parts along dimension 0
There are 4 independent parts. A program takes and returns all parts, laid end to end along the dimension named above; an argument that names none is the same for every part.
All inputs are finite; a program needn't handle non-finite values.
Results may differ from a plain program's by a relative error of at most 0.02.
Values are sent between devices in bfloat16 or wider.
A program may use at most 768 MiB of HBM per device.

v0:
```python
import jax
import jax.numpy as jnp
from jax import lax
from jax.sharding import PartitionSpec as P

ROPE_THETA = 500000.0
NORM_EPS = 1e-6


def rms_factor(sq_sum, full_width):
    return lax.rsqrt(sq_sum / full_width + NORM_EPS)


def rope_tables(positions, head_dim):
    half_dim = head_dim // 2
    inv_freq = ROPE_THETA ** (-(jnp.arange(half_dim, dtype=jnp.float32) * (2.0 / head_dim)))
    angles = positions.astype(jnp.float32)[:, None] * inv_freq[None, :]
    return jnp.cos(angles), jnp.sin(angles)


def apply_rope(head_vals, cos_tab, sin_tab):
    half_dim = head_vals.shape[-1] // 2
    lead_half = head_vals[..., :half_dim]
    tail_half = head_vals[..., half_dim:]
    cos_rows = cos_tab[:, None, :]
    sin_rows = sin_tab[:, None, :]
    return jnp.concatenate([lead_half * cos_rows - tail_half * sin_rows, tail_half * cos_rows + lead_half * sin_rows], axis=-1)


def attend(q_rot, k_old, v_old, lengths, new_keys, new_vals):
    score_scale = q_rot.shape[-1] ** -0.5
    seq_max = k_old.shape[2]
    old_scores = jnp.einsum('bkgd,bksd->bkgs', q_rot, k_old, preferred_element_type=jnp.float32) * score_scale
    old_valid = jnp.arange(seq_max)[None, :] < lengths[:, None]
    old_scores = jnp.where(old_valid[:, None, None, :], old_scores, -jnp.inf)
    new_scores = jnp.einsum('bkgd,bktd->bkgt', q_rot, new_keys, preferred_element_type=jnp.float32) * score_scale
    row_max = jnp.maximum(jnp.max(old_scores, axis=-1, keepdims=True), jnp.max(new_scores, axis=-1, keepdims=True))
    old_exp = jnp.exp(old_scores - row_max)
    new_exp = jnp.exp(new_scores - row_max)
    row_sum = jnp.sum(old_exp, axis=-1, keepdims=True) + jnp.sum(new_exp, axis=-1, keepdims=True)
    mixed_vals = jnp.einsum('bkgs,bksd->bkgd', old_exp.astype(jnp.bfloat16), v_old, preferred_element_type=jnp.float32) + jnp.einsum('bkgt,bktd->bkgd', new_exp.astype(jnp.bfloat16), new_vals, preferred_element_type=jnp.float32)
    return (mixed_vals / row_sum).astype(jnp.bfloat16)


def group_psum(part_val):
    return lax.psum(part_val, 'tp')


def layer_steps(x_seq, cache_len, k_cache, v_cache, w_q, w_k, w_v, w_o, w_gate, w_up, w_down, g_q, g_k, g_attn, g_mlp, q_width, kv_width, group_sum):
    num_steps, n_rows, d_model = x_seq.shape
    kv_loc = k_cache.shape[1]
    head_dim = k_cache.shape[-1]
    q_loc = w_q.shape[1] // head_dim
    group_size = q_loc // kv_loc
    gain_q = g_q.astype(jnp.float32)
    gain_k = g_k.astype(jnp.float32)
    gain_a = g_attn.astype(jnp.float32)
    gain_m = g_mlp.astype(jnp.float32)
    new_keys = []
    new_vals = []
    y_list = []
    for step_idx in range(num_steps):
        x_tok = x_seq[step_idx]
        positions = cache_len + step_idx
        q_raw = jnp.dot(x_tok, w_q, preferred_element_type=jnp.float32).astype(jnp.bfloat16).astype(jnp.float32)
        k_raw = jnp.dot(x_tok, w_k, preferred_element_type=jnp.float32).astype(jnp.bfloat16).astype(jnp.float32)
        v_new = jnp.dot(x_tok, w_v, preferred_element_type=jnp.float32).astype(jnp.bfloat16)
        q_sq = group_sum(jnp.sum(q_raw * q_raw, axis=-1, keepdims=True))
        k_sq = group_sum(jnp.sum(k_raw * k_raw, axis=-1, keepdims=True))
        cos_tab, sin_tab = rope_tables(positions, head_dim)
        q_normed = (q_raw * rms_factor(q_sq, q_width) * gain_q).reshape(n_rows, q_loc, head_dim)
        k_normed = (k_raw * rms_factor(k_sq, kv_width) * gain_k).reshape(n_rows, kv_loc, head_dim)
        q_rot = apply_rope(q_normed, cos_tab, sin_tab).astype(jnp.bfloat16).reshape(n_rows, kv_loc, group_size, head_dim)
        new_keys.append(apply_rope(k_normed, cos_tab, sin_tab).astype(jnp.bfloat16))
        new_vals.append(v_new.reshape(n_rows, kv_loc, head_dim))
        attn_vals = attend(q_rot, k_cache, v_cache, cache_len, jnp.stack(new_keys, axis=2), jnp.stack(new_vals, axis=2))
        attn_part = jnp.dot(attn_vals.reshape(n_rows, q_loc * head_dim), w_o, preferred_element_type=jnp.float32).astype(jnp.bfloat16)
        attn_sum = group_sum(attn_part).astype(jnp.float32)
        hidden = (x_tok.astype(jnp.float32) + attn_sum * rms_factor(jnp.sum(attn_sum * attn_sum, axis=-1, keepdims=True), d_model) * gain_a).astype(jnp.bfloat16)
        gate_pre = jnp.dot(hidden, w_gate, preferred_element_type=jnp.float32)
        up_pre = jnp.dot(hidden, w_up, preferred_element_type=jnp.float32)
        act_loc = (jax.nn.silu(gate_pre) * up_pre).astype(jnp.bfloat16)
        mlp_part = jnp.dot(act_loc, w_down, preferred_element_type=jnp.float32).astype(jnp.bfloat16)
        mlp_sum = group_sum(mlp_part).astype(jnp.float32)
        y_tok = (hidden.astype(jnp.float32) + mlp_sum * rms_factor(jnp.sum(mlp_sum * mlp_sum, axis=-1, keepdims=True), d_model) * gain_m).astype(jnp.bfloat16)
        y_list.append(y_tok)
    offsets = jnp.arange(k_cache.shape[2], dtype=jnp.int32)[None, None, :, None] - cache_len[:, None, None, None]
    k_out = k_cache
    v_out = v_cache
    for step_idx in range(num_steps):
        at_slot = offsets == step_idx
        k_out = jnp.where(at_slot, new_keys[step_idx][:, :, None, :], k_out)
        v_out = jnp.where(at_slot, new_vals[step_idx][:, :, None, :], v_out)
    return jnp.stack(y_list), k_out, v_out


def solution(mesh):
    tp_size = mesh.shape['tp']

    def local_run(x_seq, cache_len, k_cache, v_cache, w_q, w_k, w_v, w_o, w_gate, w_up, w_down, g_q, g_k, g_attn, g_mlp):
        return layer_steps(x_seq, cache_len, k_cache, v_cache, w_q, w_k, w_v, w_o, w_gate, w_up, w_down, g_q, g_k, g_attn, g_mlp, w_q.shape[1] * tp_size, w_k.shape[1] * tp_size, group_psum)

    data_spec = P(None, 'dp', None)
    cache_spec = P('dp', 'tp', None, None)
    col_spec = P(None, 'tp')
    row_spec = P('tp', None)
    arg_specs = (data_spec, P('dp'), cache_spec, cache_spec, col_spec, col_spec, col_spec, row_spec, col_spec, col_spec, row_spec, P('tp'), P('tp'), P(None), P(None))
    out_specs = (data_spec, cache_spec, cache_spec)
    return jax.shard_map(local_run, mesh=mesh, in_specs=arg_specs, out_specs=out_specs, check_vma=False)
```

profile of v0, /device:TPU:81, one launch (start us, length us, event | category | flops | bytes accessed | tf_op | source)
XLA Modules:
  0.0 287.2 jit_solution(690437378257056184)
XLA Ops:
  7.3 1.1 copy-done
  8.4 2.0 convolution_convert_fusion.9
  10.4 1.7 convolution_convert_fusion.11
  16.0 0.8 multiply_reduce_fusion.1
  16.9 14.4 %all-reduce = (f32[128,1]{0,1:T(1,128)S(1)}, f32[128,1]{0,1:T(1,128)S(1)}, f32[128,1]{0,1:T(1,128)S(1)}, f32[128,1]{0,1:T(1,128)S(1)}, f32[128,1]{0,1:T(1,128)S(1)}, /*index=5*/f32[128,1]{0,1:T(1,128)S(1)}) all-reduce(f32[128,1]{0,1:T(1,128)S(1)} %bitcast.211, f32[128,1]{0,1:T(1,128)S(1)} %bitcast.208, ...), channel_id=1, replica_groups=mesh['dp'=4,'tp'=8] {'tp'}, use_global_device_ids=true, to_apply=%region_23.24 | all-reduce | flops 768 | bytes 6144 | tf_op jit(solution)/shard_map/psum | solution.py:46
  34.0 5.9 %fusion.163 = (f32[128,4]{1,0:T(8,128)S(1)}, f32[128,4,256]{2,1,0:T(4,128)S(1)}) fusion(bf16[128,1,256,128]{3,2,1,0:T(8,128)(2,1)} %param.17, bf16[128,4,64]{2,1,0:T(4,128)(2,1)S(1)} %get-tuple-element.21, bf16[128,4,64]{2,1,0:T(4,128)(2,1)S(1)} %get-tuple-element.20, pred[128,256]{1,0:T(8,128)(4,1)S(1)} %get-tuple-element.51), kind=kOutput, calls=%fused_computation.242 | convolution fusion | flops 34209280 | bytes 9078784 | tf_op jit(solution)/shard_map/bkgd,bksd->bkgs/dot_general | solution.py:33
  40.2 5.9 %fusion.161 = (f32[128,4]{1,0:T(8,128)S(1)}, f32[128,4,256]{2,1,0:T(4,128)S(1)}) fusion(bf16[128,1,256,128]{3,2,1,0:T(8,128)(2,1)} %param.17, bf16[128,4,64]{2,1,0:T(4,128)(2,1)S(1)} %get-tuple-element.23, bf16[128,4,64]{2,1,0:T(4,128)(2,1)S(1)} %get-tuple-element.22, pred[128,256]{1,0:T(8,128)(4,1)S(1)} %get-tuple-element.51), kind=kOutput, calls=%fused_computation.240 | convolution fusion | flops 34209280 | bytes 9078784 | tf_op jit(solution)/shard_map/bkgd,bksd->bkgs/dot_general | solution.py:33
  47.0 1.2 fusion
  48.7 1.2 fusion.2
  50.7 5.7 %fusion.165 = (f32[128,4]{1,0:T(8,128)S(1)}, f32[128,4,256]{2,1,0:T(4,128)S(1)}) fusion(bf16[128,4,128]{2,1,0:T(4,128)(2,1)S(1)} %pad_maximum_fusion.1, bf16[128,1,256,128]{3,2,1,0:T(8,128)(2,1)} %param.17, pred[128,256]{1,0:T(8,128)(4,1)S(1)} %get-tuple-element.51), kind=kOutput, calls=%fused_computation.244 | convolution fusion | flops 33947136 | bytes 9078784 | tf_op jit(solution)/shard_map/bkgd,bksd->bkgs/dot_general | solution.py:33
  57.7 5.0 %fusion.61 = bf16[128,4,128]{2,1,0:T(4,128)(2,1)S(1)} fusion(bf16[128,1,256,128]{3,2,1,0:T(8,128)(2,1)} %param.18, f32[128,4,256]{2,1,0:T(4,128)S(1)} %get-tuple-element.87, f32[128,4]{1,0:T(8,128)S(1)} %multiply_maximum_fusion, f32[128,4]{1,0:T(8,128)S(1)} %get-tuple-element.25, f32[128,128]{1,0:T(8,128)S(1)} %get-tuple-element.88, ...), kind=kOutput, calls=%fused_computation.81 | convolution fusion | flops 34078720 | bytes 9115648 | tf_op jit(solution)/shard_map/bkgs,bksd->bkgd/dot_general | solution.py:41
  62.7 1.7 convolution_convert_fusion.5
  64.7 1.7 convolution_convert_fusion.3
  66.9 1.7 convolution_convert_fusion.1
  69.1 63.3 %all-reduce.8.cloned.1.call-done = (bf16[128,4096]{1,0:T(8,128)(2,1)}, bf16[128,4096]{1,0:T(8,128)(2,1)}, bf16[128,4096]{1,0:T(8,128)(2,1)}) async-done(((bf16[128,4096]{1,0:T(8,128)(2,1)}, bf16[128,4096]{1,0:T(8,128)(2,1)}, bf16[128,4096]{1,0:T(8,128)(2,1)}), (bf16[128,4096]{1,0:T(8,128)(2,1)}, bf16[128,4096]{1,0:T(8,128)(2,1)}, bf16[128,4096]{1,0:T(8,128)(2,1)})) %all-reduce.8.cloned.1.call-update) | async-done | bytes 3145744 | tf_op jit(solution)/shard_map/psum | solution.py:46
  132.4 1.5 fusion.31
  134.0 1.5 fusion.23
  135.5 1.5 fusion.15
  137.0 4.5 %fusion.18 = (bf16[128,4096]{1,0:T(8,128)(2,1)S(1)}, bf16[128,4096]{1,0:T(8,128)(2,1)S(1)}, bf16[128,4096]{1,0:T(8,128)(2,1)S(1)}) fusion(bf16[128,4096]{1,0:T(8,128)(2,1)} %get-tuple-element.14, f32[4096]{0:T(1024)S(1)} %convert_element_type.243, f32[128]{0:T(128)S(1)} %add_rsqrt_fusion.5, bf16[3,128,4096]{2,1,0:T(8,128)(2,1)} %param.15, ...), kind=kLoop, calls=%fused_computation.42 | loop fusion | flops 9437184 | bytes 9455104 | tf_op jit(solution)/shard_map/convert_element_type | solution.py:79
  141.6 8.6 %fusion.168 = f32[128,1792]{1,0:T(8,128)} fusion(bf16[128,4096]{1,0:T(8,128)(2,1)S(1)} %get-tuple-element.15, bf16[4096,1792]{1,0:T(8,128)(2,1)} %param.23), kind=kOutput, calls=%fused_computation.247 | convolution fusion | flops 1879048192 | bytes 16646144 | tf_op jit(solution)/shard_map/dot_general | solution.py:80
  150.2 3.1 %fusion.169 = f32[128,1792]{1,0:T(8,128)} fusion(bf16[128,4096]{1,0:T(8,128)(2,1)S(1)} %get-tuple-element.16, bf16[4096,1792]{1,0:T(8,128)(2,1)S(1)} %bitcast.178), kind=kOutput, calls=%fused_computation.248 | convolution fusion | flops 1879048192 | bytes 16646144 | tf_op jit(solution)/shard_map/dot_general | solution.py:80
  153.4 15.1 %convolution_convert_fusion.4 = bf16[128,4096]{1,0:T(8,128)(2,1)} fusion(bf16[1792,4096]{1,0:T(8,128)(2,1)} %param.25, bf16[128,4096]{1,0:T(8,128)(2,1)S(1)} %get-tuple-element.15, bf16[4096,1792]{1,0:T(8,128)(2,1)} %param.24, f32[128,1792]{1,0:T(8,128)} %fusion.168), kind=kOutput, calls=%fused_computation.18 | convolution fusion | flops 3759996928 | bytes 32374784 | tf_op jit(solution)/shard_map/dot_general | solution.py:83
  168.5 15.3 %convolution_convert_fusion.2 = bf16[128,4096]{1,0:T(8,128)(2,1)} fusion(bf16[1792,4096]{1,0:T(8,128)(2,1)} %param.25, bf16[128,4096]{1,0:T(8,128)(2,1)S(1)} %get-tuple-element.16, bf16[4096,1792]{1,0:T(8,128)(2,1)} %param.24, f32[128,1792]{1,0:T(8,128)} %fusion.169), kind=kOutput, calls=%fused_computation.16 | convolution fusion | flops 3759996928 | bytes 32374784 | tf_op jit(solution)/shard_map/dot_general | solution.py:83
  183.7 8.2 %fusion.170 = f32[128,1792]{1,0:T(8,128)} fusion(bf16[128,4096]{1,0:T(8,128)(2,1)S(1)} %get-tuple-element.17, bf16[4096,1792]{1,0:T(8,128)(2,1)} %param.23), kind=kOutput, calls=%fused_computation.249 | convolution fusion | flops 1879048192 | bytes 16646144 | tf_op jit(solution)/shard_map/dot_general | solution.py:80
  191.9 15.0 %convolution_convert_fusion = bf16[128,4096]{1,0:T(8,128)(2,1)} fusion(bf16[1792,4096]{1,0:T(8,128)(2,1)} %param.25, bf16[128,4096]{1,0:T(8,128)(2,1)S(1)} %get-tuple-element.17, bf16[4096,1792]{1,0:T(8,128)(2,1)} %param.24, f32[128,1792]{1,0:T(8,128)} %fusion.170), kind=kOutput, calls=%fused_computation.14 | convolution fusion | flops 3759996928 | bytes 32374784 | tf_op jit(solution)/shard_map/dot_general | solution.py:83
  207.0 18.2 %select_select_fusion = (bf16[128,1,256,128]{3,2,1,0:T(8,128)(2,1)}, bf16[128,1,256,128]{3,2,1,0:T(8,128)(2,1)}) fusion(bf16[128,1,256,128]{3,2,1,0:T(8,128)(2,1)} %param.18, pred[128,256]{1,0:T(8,128)(4,1)S(1)} %get-tuple-element.49, pred[128,256]{1,0:T(8,128)(4,1)S(1)} %get-tuple-element.50, pred[128,256]{1,0:T(8,128)(4,1)S(1)} %get-tuple-element.48, ...), kind=kLoop, calls=%fused_computation.12 | loop fusion | flops 25165824 | bytes 33849344 | tf_op jit(solution)/shard_map/jit(_where)/select_n | solution.py:93
  225.2 44.5 %all-reduce.6.cloned.1.call-done = (bf16[128,4096]{1,0:T(8,128)(2,1)}, bf16[128,4096]{1,0:T(8,128)(2,1)}, bf16[128,4096]{1,0:T(8,128)(2,1)}) async-done(((bf16[128,4096]{1,0:T(8,128)(2,1)}, bf16[128,4096]{1,0:T(8,128)(2,1)}, bf16[128,4096]{1,0:T(8,128)(2,1)}), (bf16[128,4096]{1,0:T(8,128)(2,1)}, bf16[128,4096]{1,0:T(8,128)(2,1)}, bf16[128,4096]{1,0:T(8,128)(2,1)})) %all-reduce.6.cloned.1.call-update) | async-done | bytes 3145744 | tf_op jit(solution)/shard_map/psum | solution.py:46
  269.7 1.5 fusion.35
  271.2 1.5 fusion.27
  272.8 1.5 fusion.19
  274.3 3.8 %fusion.78 = (bf16[1,128,4096]{2,1,0:T(8,128)(2,1)S(1)}, bf16[1,128,4096]{2,1,0:T(8,128)(2,1)S(1)}, bf16[1,128,4096]{2,1,0:T(8,128)(2,1)S(1)}) fusion(bf16[128,4096]{1,0:T(8,128)(2,1)} %get-tuple-element.11, bf16[128,4096]{1,0:T(8,128)(2,1)S(1)} %get-tuple-element.15, f32[4096]{0:T(1024)S(1)} %convert_element_type.249, f32[128]{0:T(128)S(1)} %add_rsqrt_fusion.4, ...), kind=kLoop, calls=%fused_computation.97 | loop fusion | flops 9437184 | bytes 9455104 | tf_op jit(solution)/shard_map/stack | solution.py:94
  278.1 2.0 pad_maximum_fusion
  (103 shorter events, 11.4 us)
Async XLA Ops:
  7.2 1.2 copy-start
  7.2 4.9 %copy-start.6 = (bf16[4096,128]{1,0:T(8,128)(2,1)S(1)}, bf16[4096,128]{1,0:T(8,128)(2,1)}, u32[]{:S(2)}) copy-start(bf16[4096,128]{1,0:T(8,128)(2,1)} %param.20) | copy-start | bytes 3145732
  7.2 125.2 %all-reduce.8.cloned.1.call-start = ((), (), s32[]{:S(2)}) async-start(), calls=%async_computation.1 | async-start | bytes 6291456 | tf_op jit(solution)/shard_map/psum | solution.py:46
  7.3 4.8 %copy-start.4 = (bf16[3,128,4096]{2,1,0:T(8,128)(2,1)S(1)}, bf16[3,128,4096]{2,1,0:T(8,128)(2,1)}, u32[]{:S(2)}) copy-start(bf16[3,128,4096]{2,1,0:T(8,128)(2,1)} %param.15) | copy-start | bytes 9437188
  12.1 2.2 copy-start.9
  12.1 2.3 copy-start.2
  15.2 1.6 copy-start.11
  15.2 1.6 copy-start.10
  34.0 13.0 %slice-start.4 = ((s8[8388608]{0:T(1024)(128)(4,1)}), s8[4194304]{0:T(1024)(128)(4,1)S(1)}, s32[]{:S(2)}) async-start(s8[8388608]{0:T(1024)(128)(4,1)} %bitcast.179), calls=%async_computation.6 | async-start | bytes 8388608
  40.2 6.8 %slice-start.5 = ((s8[8388608]{0:T(1024)(128)(4,1)}), s8[4194304]{0:T(1024)(128)(4,1)S(1)}, s32[]{:S(2)}) async-start(s8[8388608]{0:T(1024)(128)(4,1)} %bitcast.179), calls=%async_computation.7 | async-start | bytes 8388608
  57.6 5.0 %copy-start.3 = (bf16[512,4096]{1,0:T(8,128)(2,1)S(1)}, bf16[512,4096]{1,0:T(8,128)(2,1)}, u32[]{:S(2)}) copy-start(bf16[512,4096]{1,0:T(8,128)(2,1)} %param.22) | copy-start | bytes 12582916
  66.8 1.9 copy-start.7
  66.8 1.9 copy-start.8
  68.6 201.1 %all-reduce.6.cloned.1.call-start = ((), (), s32[]{:S(2)}) async-start(), calls=%async_computation | async-start | bytes 6291456 | tf_op jit(solution)/shard_map/psum | solution.py:46
  137.0 13.2 %slice-start = ((s8[14680064]{0:T(1024)(128)(4,1)}), s8[4194304]{0:T(1024)(128)(4,1)S(1)}, s32[]{:S(2)}) async-start(s8[14680064]{0:T(1024)(128)(4,1)} %bitcast.177), calls=%async_computation.2 | async-start | bytes 8388608
  137.0 13.2 %slice-start.1 = ((s8[14680064]{0:T(1024)(128)(4,1)}), s8[2097152]{0:T(1024)(128)(4,1)S(1)}, s32[]{:S(2)}) async-start(s8[14680064]{0:T(1024)(128)(4,1)} %bitcast.177), calls=%async_computation.3 | async-start | bytes 4194304
  141.6 50.3 %copy-start.5 = (bf16[128,4096]{1,0:T(8,128)(2,1)}, bf16[128,4096]{1,0:T(8,128)(2,1)S(1)}, u32[]{:S(2)}) copy-start(bf16[128,4096]{1,0:T(8,128)(2,1)S(1)} %get-tuple-element.17) | copy-start | bytes 3145732
  141.6 8.6 %slice-start.2 = ((s8[14680064]{0:T(1024)(128)(4,1)}), s8[4194304]{0:T(1024)(128)(4,1)S(1)}, s32[]{:S(2)}) async-start(s8[14680064]{0:T(1024)(128)(4,1)} %bitcast.177), calls=%async_computation.4 | async-start | bytes 8388608
  141.6 8.6 %slice-start.3 = ((s8[14680064]{0:T(1024)(128)(4,1)}), s8[4194304]{0:T(1024)(128)(4,1)S(1)}, s32[]{:S(2)}) async-start(s8[14680064]{0:T(1024)(128)(4,1)} %bitcast.177), calls=%async_computation.5 | async-start | bytes 8388608
  274.3 5.8 %copy-start.1 = (bf16[4096,128]{1,0:T(8,128)(2,1)S(1)}, bf16[4096,128]{1,0:T(8,128)(2,1)}, u32[]{:S(2)}) copy-start(bf16[4096,128]{1,0:T(8,128)(2,1)} %param.21) | copy-start | bytes 3145732
Sparse Core Ops, SparseCore 0:
  68.7 63.6 all-reduce.7
  207.1 62.5 all-reduce.5
where the time goes:
time: 292 us; the launch traced here: 287 us
  waiting for transfers between devices  108 us (37%)
  matrix products  105 us (36%)
  other arithmetic  42.2 us (14%)
  between operations  15 us (5%)
  blocking collectives  14.4 us (5%)
    psum x2, waiting for transfers between devices, group_psum(): return lax.psum(part_val, 'tp')  108 us
    dot_general x3, matrix products, layer_steps(): jnp.dot(act_loc, w_down, preferred_element_type=jnp.float32)  45.4 us
    dot_general x3, matrix products, layer_steps(): gate_pre = jnp.dot(hidden, w_gate, preferred_element_type=jnp.float32)  19.9 us
    select_n x1, other arithmetic, layer_steps(): v_out = jnp.where(at_slot, new_vals[step_idx][:, :, None, :], v_out)  18.2 us
    dot_general x3, matrix products, attend(): jnp.einsum('bkgd,bksd->bkgs', q_rot, k_old, preferred_element_type=jnp.fl...  17.6 us
    psum x1, blocking collectives, group_psum(): return lax.psum(part_val, 'tp')  14.4 us
    dot_general x3, matrix products, attend(): jnp.einsum('bkgs,bksd->bkgd', old_exp.astype(jnp.bfloat16), v_old, prefer...  7.49 us
  transfers between devices with their start and end apart: 2, of which 2 were waited for; matrix products, arithmetic and copies ran while one was open for 6% of the time, Pallas kernels for 0%

commit v1 on v0

v1 whole, which is shorter than its diff:
```python
import jax
import jax.numpy as jnp
from jax import lax
from jax.sharding import PartitionSpec as P

ROPE_THETA = 500000.0
NORM_EPS = 1e-6


def rms_factor(sq_sum, full_width):
    return lax.rsqrt(sq_sum / full_width + NORM_EPS)


def rope_tables(positions, head_dim):
    half_dim = head_dim // 2
    inv_freq = ROPE_THETA ** (-(jnp.arange(half_dim, dtype=jnp.float32) * (2.0 / head_dim)))
    angles = positions.astype(jnp.float32)[:, None] * inv_freq[None, :]
    return jnp.cos(angles), jnp.sin(angles)


def apply_rope(head_vals, cos_tab, sin_tab):
    half_dim = head_vals.shape[-1] // 2
    lead_half = head_vals[..., :half_dim]
    tail_half = head_vals[..., half_dim:]
    cos_rows = cos_tab[:, None, :]
    sin_rows = sin_tab[:, None, :]
    return jnp.concatenate([lead_half * cos_rows - tail_half * sin_rows, tail_half * cos_rows + lead_half * sin_rows], axis=-1)


def group_psum(part_val):
    return lax.psum(part_val, 'tp')


def layer_steps(x_seq, cache_len, k_cache, v_cache, w_q, w_k, w_v, w_o, w_gate, w_up, w_down, g_q, g_k, g_attn, g_mlp, q_width, kv_width, group_sum):
    num_steps, n_rows, d_model = x_seq.shape
    kv_loc = k_cache.shape[1]
    head_dim = k_cache.shape[-1]
    seq_max = k_cache.shape[2]
    q_loc = w_q.shape[1] // head_dim
    group_size = q_loc // kv_loc
    gain_q = g_q.astype(jnp.float32)
    gain_k = g_k.astype(jnp.float32)
    gain_a = g_attn.astype(jnp.float32)
    gain_m = g_mlp.astype(jnp.float32)
    x_all = x_seq.reshape(num_steps * n_rows, d_model)
    positions = (cache_len[None, :] + jnp.arange(num_steps, dtype=cache_len.dtype)[:, None]).reshape(-1)
    q_raw = jnp.dot(x_all, w_q, preferred_element_type=jnp.float32).astype(jnp.bfloat16).astype(jnp.float32)
    k_raw = jnp.dot(x_all, w_k, preferred_element_type=jnp.float32).astype(jnp.bfloat16).astype(jnp.float32)
    v_new = jnp.dot(x_all, w_v, preferred_element_type=jnp.float32).astype(jnp.bfloat16)
    sums = group_sum(jnp.concatenate([jnp.sum(q_raw * q_raw, axis=-1, keepdims=True), jnp.sum(k_raw * k_raw, axis=-1, keepdims=True)], axis=1))
    cos_tab, sin_tab = rope_tables(positions, head_dim)
    q_normed = (q_raw * rms_factor(sums[:, :1], q_width) * gain_q).reshape(-1, q_loc, head_dim)
    k_normed = (k_raw * rms_factor(sums[:, 1:], kv_width) * gain_k).reshape(-1, kv_loc, head_dim)
    q_rot = apply_rope(q_normed, cos_tab, sin_tab).astype(jnp.bfloat16)
    k_rot = apply_rope(k_normed, cos_tab, sin_tab).astype(jnp.bfloat16)
    q_rot = q_rot.reshape(num_steps, n_rows, kv_loc, group_size, head_dim).transpose(1, 2, 0, 3, 4).reshape(n_rows, kv_loc, num_steps * group_size, head_dim)
    new_k = k_rot.reshape(num_steps, n_rows, kv_loc, head_dim)
    new_v = v_new.reshape(num_steps, n_rows, kv_loc, head_dim)
    offsets = jnp.arange(seq_max, dtype=jnp.int32)[None, None, :, None] - cache_len[:, None, None, None]
    k_out = k_cache
    v_out = v_cache
    for step_idx in range(num_steps):
        k_out = jnp.where(offsets == step_idx, new_k[step_idx][:, :, None, :], k_out)
        v_out = jnp.where(offsets == step_idx, new_v[step_idx][:, :, None, :], v_out)
    scores = jnp.einsum('bkqd,bksd->bkqs', q_rot, k_out, preferred_element_type=jnp.float32) * head_dim ** -0.5
    last = cache_len[:, None] + jnp.repeat(jnp.arange(num_steps, dtype=jnp.int32), group_size)[None, :]
    valid = jnp.arange(seq_max, dtype=jnp.int32)[None, None, :] <= last[:, :, None]
    scores = jnp.where(valid[:, None], scores, -jnp.inf)
    exps = jnp.exp(scores - jnp.max(scores, axis=-1, keepdims=True))
    mixed = jnp.einsum('bkqs,bksd->bkqd', exps.astype(jnp.bfloat16), v_out, preferred_element_type=jnp.float32)
    attn = (mixed / jnp.sum(exps, axis=-1, keepdims=True)).astype(jnp.bfloat16)
    attn = attn.reshape(n_rows, kv_loc, num_steps, group_size, head_dim).transpose(2, 0, 1, 3, 4).reshape(num_steps * n_rows, q_loc * head_dim)
    attn_sum = group_sum(jnp.dot(attn, w_o, preferred_element_type=jnp.float32).astype(jnp.bfloat16)).astype(jnp.float32)
    hidden = (x_all.astype(jnp.float32) + attn_sum * rms_factor(jnp.sum(attn_sum * attn_sum, axis=-1, keepdims=True), d_model) * gain_a).astype(jnp.bfloat16)
    gate_pre = jnp.dot(hidden, w_gate, preferred_element_type=jnp.float32)
    up_pre = jnp.dot(hidden, w_up, preferred_element_type=jnp.float32)
    act = (jax.nn.silu(gate_pre) * up_pre).astype(jnp.bfloat16)
    mlp_sum = group_sum(jnp.dot(act, w_down, preferred_element_type=jnp.float32).astype(jnp.bfloat16)).astype(jnp.float32)
    y = (hidden.astype(jnp.float32) + mlp_sum * rms_factor(jnp.sum(mlp_sum * mlp_sum, axis=-1, keepdims=True), d_model) * gain_m).astype(jnp.bfloat16)
    return y.reshape(num_steps, n_rows, d_model), k_out, v_out


def solution(mesh):
    tp_size = mesh.shape['tp']

    def local_run(x_seq, cache_len, k_cache, v_cache, w_q, w_k, w_v, w_o, w_gate, w_up, w_down, g_q, g_k, g_attn, g_mlp):
        return layer_steps(x_seq, cache_len, k_cache, v_cache, w_q, w_k, w_v, w_o, w_gate, w_up, w_down, g_q, g_k, g_attn, g_mlp, w_q.shape[1] * tp_size, w_k.shape[1] * tp_size, group_psum)

    data_spec = P(None, 'dp', None)
    cache_spec = P('dp', 'tp', None, None)
    col_spec = P(None, 'tp')
    row_spec = P('tp', None)
    arg_specs = (data_spec, P('dp'), cache_spec, cache_spec, col_spec, col_spec, col_spec, row_spec, col_spec, col_spec, row_spec, P('tp'), P('tp'), P(None), P(None))
    out_specs = (data_spec, cache_spec, cache_spec)
    return jax.shard_map(local_run, mesh=mesh, in_specs=arg_specs, out_specs=out_specs, check_vma=False)
```

time: 292 us -> 249 us (0.85); the launches traced: 287 us -> 248 us
  matrix products: 105 us -> 52.1 us
  waiting for transfers between devices: 108 us -> 126 us
  other arithmetic: 42.2 us -> 35 us
  local copies, waits for them, and re-layouts: 2.23 us -> 6.24 us
    dot_general x26 -> x7, matrix products: 85.5 us -> 41.4 us  [the longest x1 25.1 us: layer_steps(): jnp.dot(act, w_down, preferred_element_type=jnp.float32)]
    psum x2, waiting for transfers between devices: 108 us -> 126 us  [group_psum(): return lax.psum(part_val, 'tp')]
    dot_general x3 -> x1, matrix products: 19.9 us -> 10.7 us  [layer_steps(): gate_pre = jnp.dot(hidden, w_gate, preferred_element_type=jnp.float32)]
    another operation x11 -> x2, other arithmetic: 7.17 us -> 0.55 us  [the longest x2 5.79 us: layer_steps(): return (jnp.stack(y_list), k_out, v_out)]
    convert_element_type x1 -> x2, other arithmetic: 4.53 us -> 8.69 us  [the longest x1 5.21 us: layer_steps(): (hidden.astype(jnp.float32) + mlp_sum * rms_factor(jnp.sum(mlp_sum * mlp_...]
    unnamed x36 -> x30, local copies, waits for them, and re-layouts: 1.22 us -> 4.66 us
  transfers between devices with their start and end apart: 2 -> 2, of which waited for: 2 -> 2; matrix products, arithmetic and copies ran while one was open for 6% -> 0% of each run, Pallas kernels for 0% -> 0%
where the time goes in v1:
time: 249 us; the launch traced here: 248 us
  waiting for transfers between devices  126 us (51%)
  matrix products  52.1 us (21%)
  other arithmetic  35 us (14%)
  between operations  14.4 us (6%)
  blocking collectives  14 us (6%)
  local copies, waits for them, and re-layouts  6.24 us (3%)
    psum x2, waiting for transfers between devices, group_psum(): return lax.psum(part_val, 'tp')  126 us
    dot_general x1, matrix products, layer_steps(): jnp.dot(act, w_down, preferred_element_type=jnp.float32)  25.1 us
    select_n x1, other arithmetic, layer_steps(): jnp.where(offsets == step_idx, new_k[step_idx][:, :, None, :], k_out)  17 us
    psum x1, blocking collectives, group_psum(): return lax.psum(part_val, 'tp')  14 us
    dot_general x1, matrix products, layer_steps(): gate_pre = jnp.dot(hidden, w_gate, preferred_element_type=jnp.float32)  10.7 us
    convert_element_type x1, other arithmetic, layer_steps(): (hidden.astype(jnp.float32) + mlp_sum * rms_factor(jnp.sum(mlp_sum * mlp_...  5.21 us
    dot_general x1, matrix products, layer_steps(): jnp.dot(x_all, w_q, preferred_element_type=jnp.float32).astype(jnp.bfloat16)  5.15 us
  transfers between devices with their start and end apart: 2, of which 2 were waited for; matrix products, arithmetic and copies ran while one was open for 0% of the time, Pallas kernels for 0%

profile of v1, /device:TPU:81, one launch (start us, length us, event | category | flops | bytes accessed | tf_op | source)
XLA Modules:
  0.0 248.1 jit_solution(11408414472455189816)
XLA Ops:
  7.3 0.7 convert_bitcast_fusion
  8.0 0.8 fusion.36
  8.8 5.2 %multiply_reduce_fusion = (f32[384]{0:T(512)S(1)}, f32[384,512]{1,0:T(8,128)S(1)}) fusion(bf16[384,4096]{1,0:T(8,128)(2,1)} %bitcast.65, bf16[4096,512]{1,0:T(8,128)(2,1)} %param.19), kind=kOutput, calls=%fused_computation.36 | convolution fusion | flops 1611398784 | bytes 8128000 | tf_op jit(solution)/shard_map/dot_general | solution.py:47
  14.0 1.0 multiply_reduce_fusion.1
  15.1 14.0 %psum.21 = f32[384,2]{0,1:T(2,128)S(1)} all-reduce(f32[384,2]{0,1:T(2,128)S(1)} %pad_maximum_fusion.1), channel_id=1, replica_groups=mesh['dp'=4,'tp'=8] {'tp'}, use_global_device_ids=true, to_apply=%region_2.0 | all-reduce | flops 768 | bytes 6144 | tf_op jit(solution)/shard_map/psum | solution.py:31
  29.2 0.4 multiply_cosine_fusion.1
  29.7 0.4 fusion.38
  30.3 0.1 copy.33
  30.6 2.9 %convolution_convert_fusion.3 = bf16[384,128]{1,0:T(8,128)(2,1)S(1)} fusion(bf16[384,4096]{1,0:T(8,128)(2,1)} %bitcast.66, bf16[4096,128]{1,0:T(8,128)(2,1)S(1)} %copy-done.8), kind=kOutput, calls=%fused_computation.31 | convolution fusion | flops 402702336 | bytes 4292608 | tf_op jit(solution)/shard_map/dot_general | solution.py:49
  33.5 0.1 multiply_multiply_fusion
  33.6 0.3 copy.38
  34.1 0.3 maximum_bitcast_fusion
  34.5 0.3 copy.31
  35.0 17.0 %select_select_fusion.1 = (bf16[128,1,256,128]{3,2,1,0:T(8,128)(2,1)S(1)}, bf16[128,1,256,128]{3,2,1,0:T(8,128)(2,1)S(1)}) fusion(bf16[128,1,256,128]{3,2,1,0:T(8,128)(2,1)} %param.17, pred[128,256]{1,0:T(8,128)(4,1)S(1)} %get-tuple-element.20, pred[128,256]{1,0:T(8,128)(4,1)S(1)} %get-tuple-element.21, pred[128,256]{1,0:T(8,128)(4,1)S(1)} %get-tuple-element.19, ...), kind=kLoop, calls=%fused_computation.5 | loop fusion | flops 25165824 | bytes 33849344 | tf_op jit(solution)/shard_map/jit(_where)/select_n | solution.py:63
  52.0 2.4 fusion.53
  54.4 1.0 copy-done.2
  55.4 0.6 fusion.13
  56.0 1.4 fusion.20
  57.5 0.6 copy-done.3
  58.1 0.3 copy.37
  58.4 1.2 copy-done.13
  59.6 3.5 %convolution_convert_fusion.1 = bf16[384,4096]{1,0:T(8,128)(2,1)} fusion(bf16[512,4096]{1,0:T(8,128)(2,1)S(1)} %copy-done.13, bf16[48,8,4,128]{3,2,1,0:T(4,128)(2,1)S(1)} %bitcast.72), kind=kOutput, calls=%fused_computation.19 | convolution fusion | flops 1612185600 | bytes 7733248 | tf_op jit(solution)/shard_map/dot_general | solution.py:73
  63.2 0.3 all-reduce.5.cloned.1.call-start
  63.5 63.3 %all-reduce.3.cloned.1.call-done = bf16[384,4096]{1,0:T(8,128)(2,1)} async-done(((bf16[384,4096]{1,0:T(8,128)(2,1)}), bf16[384,4096]{1,0:T(8,128)(2,1)}) %all-reduce.3.cloned.1.call-update) | async-done | bytes 3145744 | tf_op jit(solution)/shard_map/psum | solution.py:31
  126.8 2.7 %fusion.4 = f32[384]{0:T(512)S(1)} fusion(bf16[384,4096]{1,0:T(8,128)(2,1)} %all-reduce.3.cloned.1.call-done), kind=kLoop, calls=%fused_computation.10 | loop fusion | flops 4718208 | bytes 3147264 | tf_op jit(solution)/shard_map/reduce_sum | solution.py:74
  129.6 3.5 %fusion.7 = bf16[384,4096]{1,0:T(8,128)(2,1)S(1)} fusion(bf16[384,4096]{1,0:T(8,128)(2,1)S(1)} %copy-done.6, f32[4096]{0:T(1024)S(1)} %convert_element_type.103, f32[384]{0:T(512)S(1)} %add_rsqrt_fusion.1, bf16[3,128,4096]{2,1,0:T(8,128)(2,1)} %param.15), kind=kLoop, calls=%fused_computation.13 | loop fusion | flops 9437184 | bytes 9455104 | tf_op jit(solution)/shard_map/convert_element_type | solution.py:74
  133.1 1.7 copy-done.5
  134.7 10.7 %fusion.54 = f32[384,1792]{1,0:T(8,128)} fusion(bf16[384,4096]{1,0:T(8,128)(2,1)S(1)} %fusion.7, bf16[4096,1792]{1,0:T(8,128)(2,1)} %param.23), kind=kOutput, calls=%fused_computation.87 | convolution fusion | flops 5637144576 | bytes 20578304 | tf_op jit(solution)/shard_map/dot_general | solution.py:75
  145.5 25.1 %convolution_convert_fusion = bf16[384,4096]{1,0:T(8,128)(2,1)} fusion(bf16[1792,4096]{1,0:T(8,128)(2,1)} %param.25, bf16[384,4096]{1,0:T(8,128)(2,1)} %copy-done.5, bf16[4096,1792]{1,0:T(8,128)(2,1)} %param.24, f32[384,1792]{1,0:T(8,128)} %fusion.54), kind=kOutput, calls=%fused_computation.18 | convolution fusion | flops 11279990784 | bytes 38404096 | tf_op jit(solution)/shard_map/dot_general | solution.py:78
  170.6 62.5 %all-reduce.5.cloned.1.call-done = bf16[384,4096]{1,0:T(8,128)(2,1)} async-done(((bf16[384,4096]{1,0:T(8,128)(2,1)}), bf16[384,4096]{1,0:T(8,128)(2,1)}) %all-reduce.5.cloned.1.call-update) | async-done | bytes 3145744 | tf_op jit(solution)/shard_map/psum | solution.py:31
  233.2 2.7 %fusion.8 = f32[384]{0:T(512)S(1)} fusion(bf16[384,4096]{1,0:T(8,128)(2,1)} %all-reduce.5.cloned.1.call-done), kind=kLoop, calls=%fused_computation.14 | loop fusion | flops 4718208 | bytes 3147264 | tf_op jit(solution)/shard_map/reduce_sum | solution.py:79
  236.0 5.2 %fusion.11 = bf16[384,4096]{1,0:T(8,128)(2,1)} fusion(bf16[384,4096]{1,0:T(8,128)(2,1)S(1)} %copy-done.7, bf16[384,4096]{1,0:T(8,128)(2,1)} %copy-done.5, f32[4096]{0:T(1024)S(1)} %convert_element_type.109, f32[384]{0:T(512)S(1)} %add_rsqrt_fusion), kind=kLoop, calls=%fused_computation.17 | loop fusion | flops 9437184 | bytes 9455104 | tf_op jit(solution)/shard_map/convert_element_type | solution.py:79
  (52 shorter events, 1.3 us)
Async XLA Ops:
  7.2 6.8 %copy-start = (bf16[4096,128]{1,0:T(8,128)(2,1)S(1)}, bf16[4096,128]{1,0:T(8,128)(2,1)}, u32[]{:S(2)}) copy-start(bf16[4096,128]{1,0:T(8,128)(2,1)} %param.20) | copy-start | bytes 3145732
  7.2 119.6 %all-reduce.3.cloned.1.call-start = ((), (), s32[]{:S(2)}) async-start(), calls=%async_computation | async-start | bytes 6291456 | tf_op jit(solution)/shard_map/psum | solution.py:31
  8.8 5.2 %copy-start.4 = (bf16[3,128,4096]{2,1,0:T(8,128)(2,1)S(1)}, bf16[3,128,4096]{2,1,0:T(8,128)(2,1)}, u32[]{:S(2)}) copy-start(bf16[3,128,4096]{2,1,0:T(8,128)(2,1)} %param.15) | copy-start | bytes 9437188
  14.0 15.2 %copy-start.14 = (bf16[128]{0:T(256)(128)(2,1)S(1)}, bf16[128]{0:T(256)(128)(2,1)}, u32[]{:S(2)}) copy-start(bf16[128]{0:T(256)(128)(2,1)} %param.27) | copy-start | bytes 772
  14.0 16.6 %copy-start.8 = (bf16[4096,128]{1,0:T(8,128)(2,1)S(1)}, bf16[4096,128]{1,0:T(8,128)(2,1)}, u32[]{:S(2)}) copy-start(bf16[4096,128]{1,0:T(8,128)(2,1)} %param.21) | copy-start | bytes 3145732
  14.0 19.5 %copy-start.12 = (bf16[512]{0:T(512)(128)(2,1)S(1)}, bf16[512]{0:T(512)(128)(2,1)}, u32[]{:S(2)}) copy-start(bf16[512]{0:T(512)(128)(2,1)} %param.26) | copy-start | bytes 3076
  33.4 1.5 copy-start.11
  52.0 3.4 %copy-start.2 = (bf16[128,1,256,128]{3,2,1,0:T(8,128)(2,1)}, bf16[128,1,256,128]{3,2,1,0:T(8,128)(2,1)S(1)}, u32[]{:S(2)}) copy-start(bf16[128,1,256,128]{3,2,1,0:T(8,128)(2,1)S(1)} %get-tuple-element.9) | copy-start | bytes 25165828
  52.0 6.1 %copy-start.3 = (bf16[128,1,256,128]{3,2,1,0:T(8,128)(2,1)}, bf16[128,1,256,128]{3,2,1,0:T(8,128)(2,1)S(1)}, u32[]{:S(2)}) copy-start(bf16[128,1,256,128]{3,2,1,0:T(8,128)(2,1)S(1)} %get-tuple-element.10) | copy-start | bytes 25165828
  56.0 3.6 %copy-start.13 = (bf16[512,4096]{1,0:T(8,128)(2,1)S(1)}, bf16[512,4096]{1,0:T(8,128)(2,1)}, u32[]{:S(2)}) copy-start(bf16[512,4096]{1,0:T(8,128)(2,1)} %param.22) | copy-start | bytes 12582916
  59.6 3.8 %copy-start.9 = (bf16[4096]{0:T(1024)(128)(2,1)S(1)}, bf16[4096]{0:T(1024)(128)(2,1)}, u32[]{:S(2)}) copy-start(bf16[4096]{0:T(1024)(128)(2,1)} %param.28) | copy-start | bytes 24580
  63.2 170.0 %all-reduce.5.cloned.1.call-start = ((), (), s32[]{:S(2)}) async-start(), calls=%async_computation.1 | async-start | bytes 6291456 | tf_op jit(solution)/shard_map/psum | solution.py:31
  126.8 2.8 %copy-start.6 = (bf16[384,4096]{1,0:T(8,128)(2,1)S(1)}, bf16[384,4096]{1,0:T(8,128)(2,1)}, u32[]{:S(2)}) copy-start(bf16[384,4096]{1,0:T(8,128)(2,1)} %all-reduce.3.cloned.1.call-done) | copy-start | bytes 9437188
  133.1 1.7 copy-start.5
  145.5 25.1 %copy-start.10 = (bf16[4096]{0:T(1024)(128)(2,1)S(1)}, bf16[4096]{0:T(1024)(128)(2,1)}, u32[]{:S(2)}) copy-start(bf16[4096]{0:T(1024)(128)(2,1)} %param.29) | copy-start | bytes 24580
  233.2 2.8 %copy-start.7 = (bf16[384,4096]{1,0:T(8,128)(2,1)S(1)}, bf16[384,4096]{1,0:T(8,128)(2,1)}, u32[]{:S(2)}) copy-start(bf16[384,4096]{1,0:T(8,128)(2,1)} %all-reduce.5.cloned.1.call-done) | copy-start | bytes 9437188
  235.9 5.3 %copy-start.1 = (bf16[4096,128]{1,0:T(8,128)(2,1)S(1)}, bf16[4096,128]{1,0:T(8,128)(2,1)}, u32[]{:S(2)}) copy-start(bf16[4096,128]{1,0:T(8,128)(2,1)} %param.20) | copy-start | bytes 3145732
Sparse Core Ops, SparseCore 0:
  63.3 63.4 all-reduce.2
  170.7 62.3 all-reduce.4

commit v2 on v1

v2 whole, which is shorter than its diff:
```python
import functools

import jax
import jax.numpy as jnp
import numpy as np
from jax import lax
from jax.experimental import pallas as pl
from jax.experimental.pallas import tpu as pltpu
from jax.sharding import PartitionSpec as P

ROPE_THETA = 500000.0
NORM_EPS = 1e-6
F32 = jnp.float32
BF16 = jnp.bfloat16
MESH = pl.DeviceIdType.MESH
VMEM_SPEC = pl.BlockSpec(memory_space=pltpu.VMEM)
ANY_SPEC = pl.BlockSpec(memory_space=pl.ANY)
SMEM_SPEC = pl.BlockSpec(memory_space=pltpu.SMEM)
VMEM_LIMIT = 67043328
SLOT_ROWS = 16


def matmul(lhs, rhs):
    return jnp.dot(lhs, rhs, preferred_element_type=F32)


def qkv_kernel(tp, q_width, kv_width, x_hbm, len_ref, freq_ref, wq_hbm, wk_hbm, wv_hbm, gq_ref, gk_ref,
               q_out, kn_out, vn_out,
               x_buf, wq_buf, wk_buf, wv_buf, q_raw, q_rows, part, inbox, turn, in_sem, send_sem, recv_sem):
    steps, rows, _ = x_hbm.shape
    hd = wk_hbm.shape[1]
    heads = wq_hbm.shape[1] // hd
    pad = q_out.shape[1]
    me = lax.axis_index("tp")
    x_in = [pltpu.make_async_copy(x_hbm.at[t], x_buf.at[pl.ds(t * rows, rows), :], in_sem.at[t]) for t in range(steps)]
    for copy in x_in:
        copy.start()
    half = heads * hd // 2
    wk_in = pltpu.make_async_copy(wk_hbm, wk_buf, in_sem.at[3])
    wq_in = [pltpu.make_async_copy(wq_hbm.at[:, pl.ds(j * half, half)], wq_buf.at[:, pl.ds(j * half, half)], in_sem.at[4 + j]) for j in range(2)]
    wv_in = pltpu.make_async_copy(wv_hbm, wv_buf, in_sem.at[6])
    for copy in (wk_in, wq_in[0], wq_in[1], wv_in):
        copy.start()

    barrier = pltpu.get_barrier_semaphore()
    for j in range(1, tp):
        pl.semaphore_signal(barrier, inc=1, device_id={"tp": lax.rem(me + j, tp)}, device_id_type=MESH)

    lens = jnp.transpose(jnp.broadcast_to(len_ref[...].astype(F32), (rows, rows)))[:, :hd]
    lane = lax.broadcasted_iota(jnp.int32, (rows, hd), 1)
    sign = jnp.where(lane < hd // 2, -1.0, 1.0).astype(F32)
    tables = []
    for t in range(steps):
        angle = (lens + float(t)) * freq_ref[...]
        tables.append((jnp.cos(angle), jnp.sin(angle) * sign))

    q_rows[...] = jnp.zeros_like(q_rows)
    for copy in x_in:
        copy.wait()
    wk_in.wait()
    k_raw = matmul(x_buf[...], wk_buf[...]).astype(BF16).astype(F32)
    k_sq = jnp.sum(k_raw * k_raw, axis=1, keepdims=True)
    q_sq = None
    for j in range(2):
        wq_in[j].wait()
        val = matmul(x_buf[...], wq_buf[:, j * half:(j + 1) * half]).astype(BF16).astype(F32)
        q_raw[:, j * half:(j + 1) * half] = val
        sq = jnp.sum(val * val, axis=1, keepdims=True)
        q_sq = sq if q_sq is None else q_sq + sq
    packed = jnp.zeros((rows, rows), F32)
    col = lax.broadcasted_iota(jnp.int32, (rows, rows), 1)
    for t in range(steps):
        packed = jnp.where(col == t, q_sq[t * rows:(t + 1) * rows], packed)
        packed = jnp.where(col == steps + t, k_sq[t * rows:(t + 1) * rows], packed)
    part[...] = jnp.transpose(packed)[:part.shape[0]]
    pl.semaphore_wait(barrier, tp - 1)
    copies = []
    for j in range(1, tp):
        copy = pltpu.make_async_remote_copy(
            src_ref=part, dst_ref=inbox.at[j - 1], send_sem=send_sem.at[j - 1], recv_sem=recv_sem.at[j - 1],
            device_id={"tp": lax.rem(me + j, tp)}, device_id_type=MESH)
        copy.start()
        copies.append(copy)
    wv_in.wait()
    vn_out[...] = matmul(x_buf[...], wv_buf[...]).astype(BF16).astype(F32).reshape(steps, rows, hd)
    total = part[...]
    for j in range(1, tp):
        copies[j - 1].wait()
        total = total + inbox[j - 1]
    turn[...] = jnp.zeros_like(turn)
    turn[0:part.shape[0], :] = total
    sums = jnp.transpose(turn[...])
    gain_k = gk_ref[...].astype(F32)
    for t in range(steps):
        cos_tab, sin_tab = tables[t]
        q_fac = lax.rsqrt(sums[:, t:t + 1] / q_width + NORM_EPS)
        k_fac = lax.rsqrt(sums[:, steps + t:steps + t + 1] / kv_width + NORM_EPS)
        val = k_raw[t * rows:(t + 1) * rows] * k_fac * gain_k
        val = val * cos_tab + pltpu.roll(val, hd // 2, axis=1) * sin_tab
        kn_out[t] = val.astype(BF16).astype(F32)
        for g in range(heads):
            val = q_raw[t * rows:(t + 1) * rows, g * hd:(g + 1) * hd] * q_fac * gq_ref[:, g * hd:(g + 1) * hd].astype(F32)
            val = val * cos_tab + pltpu.roll(val, hd // 2, axis=1) * sin_tab
            q_rows[pl.ds(t * heads + g, rows, stride=pad), :] = val
    q_out[...] = q_rows[...].reshape(rows, pad, hd).astype(BF16)


def run_qkv(tp, x_seq, cache_len, w_q, w_k, w_v, g_q, g_k):
    steps, rows, d_model = x_seq.shape
    hd = w_k.shape[1]
    width = w_q.shape[1]
    heads = width // hd
    pad = 16
    inv_freq = (ROPE_THETA ** (-(np.arange(hd // 2, dtype=np.float64) * (2.0 / hd)))).astype(np.float32)
    freq = jnp.asarray(np.concatenate([inv_freq, inv_freq])[None, :])
    return pl.pallas_call(
        functools.partial(qkv_kernel, tp, width * tp, hd * tp),
        out_shape=(jax.ShapeDtypeStruct((rows, pad, hd), BF16),
                   jax.ShapeDtypeStruct((steps, rows, hd), F32),
                   jax.ShapeDtypeStruct((steps, rows, hd), F32)),
        in_specs=[ANY_SPEC, VMEM_SPEC, VMEM_SPEC, ANY_SPEC, ANY_SPEC, ANY_SPEC, VMEM_SPEC, VMEM_SPEC],
        out_specs=(VMEM_SPEC, VMEM_SPEC, VMEM_SPEC),
        scratch_shapes=[
            pltpu.VMEM((steps * rows, d_model), BF16),
            pltpu.VMEM((d_model, width), BF16),
            pltpu.VMEM((d_model, hd), BF16),
            pltpu.VMEM((d_model, hd), BF16),
            pltpu.VMEM((steps * rows, width), F32),
            pltpu.VMEM((rows * pad, hd), F32),
            pltpu.VMEM((8, rows), F32),
            pltpu.VMEM((tp - 1, 8, rows), F32),
            pltpu.VMEM((rows, rows), F32),
            pltpu.SemaphoreType.DMA((7,)),
            pltpu.SemaphoreType.DMA((tp - 1,)),
            pltpu.SemaphoreType.DMA((tp - 1,)),
        ],
        compiler_params=pltpu.CompilerParams(collective_id=0, has_side_effects=True, vmem_limit_bytes=VMEM_LIMIT),
        name="qkv",
    )(x_seq, cache_len.reshape(1, rows), freq, w_q, w_k, w_v, g_q.reshape(1, width), g_k.reshape(1, hd))


SEQ_BLOCK = 8
PATCH_ROWS = 32


def attention_kernel(steps, heads, len_ref, q_ref, kn_ref, vn_ref, k_hbm, v_hbm, o_ref, k_out, v_out,
                     k_buf, v_buf, mixed, in_sem, out_sem):
    rows, seq_max, hd = k_hbm.shape
    pad = q_ref.shape[1]
    blocks = rows // SEQ_BLOCK

    def moves(blk, inward):
        sl = pl.ds(blk * SEQ_BLOCK, SEQ_BLOCK)
        if inward:
            return (pltpu.make_async_copy(k_hbm.at[sl], k_buf.at[sl], in_sem.at[0, blk]),
                    pltpu.make_async_copy(v_hbm.at[sl], v_buf.at[sl], in_sem.at[1, blk]))
        return (pltpu.make_async_copy(k_buf.at[sl], k_out.at[sl], out_sem.at[0, blk]),
                pltpu.make_async_copy(v_buf.at[sl], v_out.at[sl], out_sem.at[1, blk]))

    def start_in(blk, carry):
        for copy in moves(blk, True):
            copy.start()
        return carry

    lax.fori_loop(0, blocks, start_in, 0)
    scale = hd ** -0.5
    win_row = lax.broadcasted_iota(jnp.int32, (PATCH_ROWS, hd), 0)
    key_col = lax.broadcasted_iota(jnp.int32, (pad, seq_max), 1)
    step_row = lax.broadcasted_iota(jnp.int32, (pad, seq_max), 0) // heads
    key_off = key_col - step_row

    def body(blk, carry):
        for copy in moves(blk, True):
            copy.wait()
        lens = []
        for i in range(SEQ_BLOCK):
            b = blk * SEQ_BLOCK + i
            length = len_ref[b]
            base = pl.multiple_of(jnp.minimum((length // 16) * 16, seq_max - PATCH_ROWS), 16)
            for buf, new_ref in ((k_buf, kn_ref), (v_buf, vn_ref)):
                win = buf[b, pl.ds(base, PATCH_ROWS), :].astype(F32)
                for t in range(steps):
                    win = jnp.where(win_row == length + t - base, new_ref[t, pl.ds(b, 1), :], win)
                buf[b, pl.ds(base, PATCH_ROWS), :] = win.astype(BF16)
            lens.append(length)
        scores = []
        for i in range(SEQ_BLOCK):
            b = blk * SEQ_BLOCK + i
            s = lax.dot_general(q_ref[b], k_buf[b], (((1,), (1,)), ((), ())), preferred_element_type=F32) * scale
            scores.append(jnp.where(key_off <= lens[i], s, -jnp.inf))
        exps = []
        for i in range(SEQ_BLOCK):
            e = jnp.exp(scores[i] - jnp.max(scores[i], axis=1, keepdims=True))
            exps.append((e.astype(BF16), jnp.sum(e, axis=1, keepdims=True)))
        for i in range(SEQ_BLOCK):
            b = blk * SEQ_BLOCK + i
            out = matmul(exps[i][0], v_buf[b]) / exps[i][1]
            mixed[pl.ds(pl.multiple_of(b * pad, pad), pad), :] = out
        for copy in moves(blk, False):
            copy.start()
        return carry

    lax.fori_loop(0, blocks, body, 0)
    for t in range(steps):
        for g in range(heads):
            o_ref[t, :, g * hd:(g + 1) * hd] = mixed[pl.ds(t * heads + g, rows, stride=pad), :].astype(BF16)

    def finish(blk, carry):
        for copy in moves(blk, False):
            copy.wait()
        return carry

    lax.fori_loop(0, blocks, finish, 0)


def run_attention(heads, cache_len, q_rows, k_new, v_new, k_cache, v_cache):
    rows, _, seq_max, hd = k_cache.shape
    steps = k_new.shape[0]
    pad = q_rows.shape[1]
    flat = jax.ShapeDtypeStruct((rows, seq_max, hd), BF16)
    out, k_out, v_out = pl.pallas_call(
        functools.partial(attention_kernel, steps, heads),
        out_shape=(jax.ShapeDtypeStruct((steps, rows, heads * hd), BF16), flat, flat),
        in_specs=[SMEM_SPEC, VMEM_SPEC, VMEM_SPEC, VMEM_SPEC, ANY_SPEC, ANY_SPEC],
        out_specs=(VMEM_SPEC, ANY_SPEC, ANY_SPEC),
        scratch_shapes=[
            pltpu.VMEM((rows, seq_max, hd), BF16),
            pltpu.VMEM((rows, seq_max, hd), BF16),
            pltpu.VMEM((rows * pad, hd), F32),
            pltpu.SemaphoreType.DMA((2, rows // SEQ_BLOCK)),
            pltpu.SemaphoreType.DMA((2, rows // SEQ_BLOCK)),
        ],
        compiler_params=pltpu.CompilerParams(vmem_limit_bytes=VMEM_LIMIT),
        name="attention",
    )(cache_len, q_rows, k_new, v_new, k_cache.reshape(rows, seq_max, hd), v_cache.reshape(rows, seq_max, hd))
    return out, k_out.reshape(k_cache.shape), v_out.reshape(v_cache.shape)


COPIES = ("pair_l", "pair_r", "relay_r", "relay_l", "near_r", "near_l", "far_r", "far_l",
          "own_r", "own_l", "own_s", "pass_r", "pass_l", "sib_l", "sib_r", "sib_fl", "sib_fr")
GATE_TILE = 256
DOWN_TILE = 512


def mlp_kernel(chips, x_hbm, o_ref, wo_hbm, w1_hbm, w3_hbm, w2_hbm, ga_ref, gm_ref, y_out,
               wo, w1, w3, w2, x_own, part, pair_in, relay_in, near_in, hid, act, w_sem, x_sem, y_sem, send_sem, recv_sem):
    steps, rows, d_model = x_hbm.shape
    ff = w1_hbm.shape[1]
    half = d_model // 2
    me = lax.axis_index("tp")
    chip, core = me // 2, lax.rem(me, 2)
    nxt, prv, opp = lax.rem(chip + 1, chips), lax.rem(chip + chips - 1, chips), lax.rem(chip + 2, chips)
    right, left, sib = nxt * 2 + core, prv * 2 + core, chip * 2 + 1 - core
    lo, hi = pl.ds(0, half), pl.ds(half, half)
    n_gate, n_down = ff // GATE_TILE, d_model // DOWN_TILE

    def cols(hbm, buf, j, width, sem):
        return pltpu.make_async_copy(hbm.at[:, pl.ds(j * width, width)], buf.at[:, pl.ds(j * width, width)], w_sem.at[sem])

    wo_in = [cols(wo_hbm, wo, j, half, j) for j in range(2)]
    w1_in = [cols(w1_hbm, w1, j, GATE_TILE, 2 + j) for j in range(n_gate)]
    w3_in = [cols(w3_hbm, w3, j, GATE_TILE, 2 + n_gate + j) for j in range(n_gate)]
    w2_in = [cols(w2_hbm, w2, j, DOWN_TILE, 2 + 2 * n_gate + j) for j in range(n_down)]

    def slot(c, k):
        return pl.ds(pl.multiple_of((c * 2 + k) * SLOT_ROWS, SLOT_ROWS), SLOT_ROWS)

    x_in = [pltpu.make_async_copy(x_hbm.at[t, slot(chip, core), :], x_own.at[t], x_sem.at[t]) for t in range(steps)]
    for copy in wo_in + x_in:
        copy.start()
    for j in range(n_gate):
        w1_in[j].start()
        w3_in[j].start()
    for copy in w2_in:
        copy.start()

    barrier = pltpu.get_barrier_semaphore()
    for other in (right, left, sib):
        pl.semaphore_signal(barrier, inc=1, device_id={"tp": other}, device_id_type=MESH)
    pl.semaphore_wait(barrier, 3)

    def remote(ph, t, name, src, dst, device):
        j = COPIES.index(name)
        return pltpu.make_async_remote_copy(
            src_ref=src, dst_ref=dst, send_sem=send_sem.at[ph, t, j], recv_sem=recv_sem.at[ph, t, j],
            device_id={"tp": device}, device_id_type=MESH)

    def copy(ph, t, name):
        own, other = part.at[t, :, core], part.at[t, :, 1 - core]
        if name == "pair_l":
            return remote(ph, t, name, other.at[:, :, lo], pair_in.at[t, :, :, lo], sib)
        if name == "pair_r":
            return remote(ph, t, name, other.at[:, :, hi], pair_in.at[t, :, :, hi], sib)
        if name == "relay_r":
            return remote(ph, t, name, own.at[opp, :, lo], relay_in.at[t, 0], right)
        if name == "relay_l":
            return remote(ph, t, name, own.at[opp, :, hi], relay_in.at[t, 1], left)
        if name == "near_r":
            return remote(ph, t, name, own.at[nxt, :, hi], near_in.at[t, 0, :, hi], right)
        if name == "near_l":
            return remote(ph, t, name, own.at[prv, :, lo], near_in.at[t, 1, :, lo], left)
        if name == "far_r":
            return remote(ph, t, name, own.at[nxt, :, lo], near_in.at[t, 0, :, lo], right)
        if name == "far_l":
            return remote(ph, t, name, own.at[prv, :, hi], near_in.at[t, 1, :, hi], left)

        def block(c, c_cols, device):
            ref = hid.at[t, slot(c, core), c_cols]
            return remote(ph, t, name, ref, ref, device)

        full = pl.ds(0, d_model)
        if name == "own_r":
            return block(chip, full, right)
        if name == "own_l":
            return block(chip, full, left)
        if name == "own_s":
            return block(chip, full, sib)
        if name == "pass_r":
            return block(prv, lo, right)
        if name == "pass_l":
            return block(nxt, hi, left)
        if name == "sib_l":
            return block(prv, full, sib)
        if name == "sib_r":
            return block(nxt, full, sib)
        if name == "sib_fl":
            return block(opp, lo, sib)
        return block(opp, hi, sib)

    def send(ph, t, *names):
        for name in names:
            copy(ph, t, name).start()

    def recv(ph, t, *names):
        for name in names:
            copy(ph, t, name).wait_recv()

    def sent(ph, t, names):
        for name in names:
            copy(ph, t, name).wait_send()

    def proj(t):
        for j, name in enumerate(("pair_l", "pair_r")):
            if t == 0:
                wo_in[j].wait()
            for n in range(j * half, (j + 1) * half, DOWN_TILE):
                val = matmul(o_ref[t], wo[:, n:n + DOWN_TILE]).astype(BF16)
                part[t, :, :, :, n:n + DOWN_TILE] = val.reshape(chips, 2, SLOT_ROWS, DOWN_TILE)
            send(0, t, name)

    def pair_add(ph, t):
        recv(ph, t, "pair_l", "pair_r")
        for c in range(chips):
            part[t, c, core] = (part[t, c, core].astype(F32) + pair_in[t, c].astype(F32)).astype(BF16)
        send(ph, t, "relay_r", "relay_l", "near_r", "near_l")

    def relay_add(ph, t):
        recv(ph, t, "relay_r")
        part[t, nxt, core, :, :half] = (part[t, nxt, core, :, :half].astype(F32) + relay_in[t, 0].astype(F32)).astype(BF16)
        send(ph, t, "far_r")
        recv(ph, t, "relay_l")
        part[t, prv, core, :, half:] = (part[t, prv, core, :, half:].astype(F32) + relay_in[t, 1].astype(F32)).astype(BF16)
        send(ph, t, "far_l")

    def norm_send(ph, t):
        recv(ph, t, "near_r", "near_l", "far_r", "far_l")
        total = part[t, chip, core].astype(F32) + near_in[t, 0].astype(F32) + near_in[t, 1].astype(F32)
        total = total.astype(BF16).astype(F32)
        fac = lax.rsqrt(jnp.sum(total * total, axis=1, keepdims=True) / d_model + NORM_EPS)
        if ph == 0:
            x_in[t].wait()
            base, gain = x_own[t], ga_ref[...]
        else:
            base, gain = hid[t, slot(chip, core), :], gm_ref[...]
        hid[t, slot(chip, core), :] = (base.astype(F32) + total * fac * gain.astype(F32)).astype(BF16)
        send(ph, t, "own_r", "own_l", "own_s")

    def pass_on(ph, t):
        recv(ph, t, "own_r")
        send(ph, t, "pass_r", "sib_l")
        recv(ph, t, "own_l")
        send(ph, t, "pass_l", "sib_r")

    def pass_sib(ph, t):
        recv(ph, t, "pass_r")
        send(ph, t, "sib_fl")
        recv(ph, t, "pass_l")
        send(ph, t, "sib_fr")

    def gathered(ph, t):
        recv(ph, t, "own_s", "sib_l", "sib_r", "sib_fl", "sib_fr")

    def mlp(t, hooks):
        def run_hooks(key):
            for fn, ph, s in hooks.get(key, ()):
                fn(ph, s)

        for j in range(n_gate):
            if t == 0:
                w1_in[j].wait()
                w3_in[j].wait()
            sl = slice(j * GATE_TILE, (j + 1) * GATE_TILE)
            gate = matmul(hid[t], w1[:, sl])
            up = matmul(hid[t], w3[:, sl])
            act[:, sl] = (gate / (1.0 + jnp.exp(-gate)) * up).astype(BF16)
            run_hooks("g%d" % j)
        sent(0, t, COPIES)
        for j in range(n_down):
            if t == 0:
                w2_in[j].wait()
            sl = slice(j * DOWN_TILE, (j + 1) * DOWN_TILE)
            val = matmul(act[...], w2[:, sl]).astype(BF16)
            part[t, :, :, :, sl] = val.reshape(chips, 2, SLOT_ROWS, DOWN_TILE)
            if j == n_down // 2 - 1:
                send(1, t, "pair_l")
            if j == n_down - 1:
                send(1, t, "pair_r")
            run_hooks("d%d" % j)

    def write_y(ph, t):
        gathered(ph, t)
        pltpu.make_async_copy(hid.at[t], y_out.at[t], y_sem.at[t]).start()

    proj(0)
    proj(1)
    pair_add(0, 0)
    proj(2)
    pair_add(0, 1)
    relay_add(0, 0)
    pair_add(0, 2)
    relay_add(0, 1)
    norm_send(0, 0)
    relay_add(0, 2)
    norm_send(0, 1)
    pass_on(0, 0)
    norm_send(0, 2)
    pass_sib(0, 0)
    gathered(0, 0)
    mlp(0, {"g0": [(pass_on, 0, 1)], "g3": [(pass_sib, 0, 1)], "g5": [(pass_on, 0, 2)],
            "d3": [(pass_sib, 0, 2)], "d7": [(gathered, 0, 1)]})
    mlp(1, {"g2": [(pair_add, 1, 0)], "g6": [(relay_add, 1, 0)], "d7": [(norm_send, 1, 0), (gathered, 0, 2)]})
    mlp(2, {"g2": [(pair_add, 1, 1)], "g6": [(relay_add, 1, 1)], "d1": [(pass_on, 1, 0)], "d6": [(norm_send, 1, 1)],
            "d7": [(pass_sib, 1, 0)]})
    pair_add(1, 2)
    write_y(1, 0)
    pass_on(1, 1)
    relay_add(1, 2)
    pass_sib(1, 1)
    norm_send(1, 2)
    write_y(1, 1)
    pass_on(1, 2)
    pass_sib(1, 2)
    write_y(1, 2)
    for t in range(steps):
        sent(1, t, COPIES)
        pltpu.make_async_copy(hid.at[t], y_out.at[t], y_sem.at[t]).wait()


def run_mlp(tp, x_seq, attn, w_o, w_gate, w_up, w_down, g_attn, g_mlp):
    steps, rows, d_model = x_seq.shape
    ff = w_gate.shape[1]
    chips = tp // 2
    half = d_model // 2
    n_sem = 2 + 2 * (ff // GATE_TILE) + d_model // DOWN_TILE
    return pl.pallas_call(
        functools.partial(mlp_kernel, chips),
        out_shape=jax.ShapeDtypeStruct((steps, rows, d_model), BF16),
        in_specs=[ANY_SPEC, VMEM_SPEC, ANY_SPEC, ANY_SPEC, ANY_SPEC, ANY_SPEC, VMEM_SPEC, VMEM_SPEC],
        out_specs=ANY_SPEC,
        scratch_shapes=[
            pltpu.VMEM(w_o.shape, BF16),
            pltpu.VMEM(w_gate.shape, BF16),
            pltpu.VMEM(w_up.shape, BF16),
            pltpu.VMEM(w_down.shape, BF16),
            pltpu.VMEM((steps, SLOT_ROWS, d_model), BF16),
            pltpu.VMEM((steps, chips, 2, SLOT_ROWS, d_model), BF16),
            pltpu.VMEM((steps, chips, SLOT_ROWS, d_model), BF16),
            pltpu.VMEM((steps, 2, SLOT_ROWS, half), BF16),
            pltpu.VMEM((steps, 2, SLOT_ROWS, d_model), BF16),
            pltpu.VMEM((steps, rows, d_model), BF16),
            pltpu.VMEM((rows, ff), BF16),
            pltpu.SemaphoreType.DMA((n_sem,)),
            pltpu.SemaphoreType.DMA((steps,)),
            pltpu.SemaphoreType.DMA((steps,)),
            pltpu.SemaphoreType.DMA((2, steps, len(COPIES))),
            pltpu.SemaphoreType.DMA((2, steps, len(COPIES))),
        ],
        compiler_params=pltpu.CompilerParams(collective_id=1, has_side_effects=True, vmem_limit_bytes=VMEM_LIMIT),
        name="mlp",
    )(x_seq, attn, w_o, w_gate, w_up, w_down, g_attn.reshape(1, d_model), g_mlp.reshape(1, d_model))


def solution(mesh):
    tp = mesh.shape['tp']

    def local_run(x_seq, cache_len, k_cache, v_cache, w_q, w_k, w_v, w_o, w_gate, w_up, w_down, g_q, g_k, g_attn, g_mlp):
        heads = w_q.shape[1] // w_k.shape[1]
        q_rows, k_new, v_new = run_qkv(tp, x_seq, cache_len, w_q, w_k, w_v, g_q, g_k)
        attn, k_out, v_out = run_attention(heads, cache_len, q_rows, k_new, v_new, k_cache, v_cache)
        y_seq = run_mlp(tp, x_seq, attn, w_o, w_gate, w_up, w_down, g_attn, g_mlp)
        return y_seq, k_out, v_out

    data_spec = P(None, 'dp', None)
    cache_spec = P('dp', 'tp', None, None)
    col_spec = P(None, 'tp')
    row_spec = P('tp', None)
    arg_specs = (data_spec, P('dp'), cache_spec, cache_spec, col_spec, col_spec, col_spec, row_spec, col_spec, col_spec, row_spec, P('tp'), P('tp'), P(None), P(None))
    out_specs = (data_spec, cache_spec, cache_spec)
    return jax.shard_map(local_run, mesh=mesh, in_specs=arg_specs, out_specs=out_specs, check_vma=False)
```

time: 249 us -> 124 us (0.50)
  waiting for transfers between devices: 126 us -> 0 us
  Pallas kernels: 0 us -> 116 us
  matrix products: 52.1 us -> 0 us
  other arithmetic: 35 us -> 0 us
  blocking collectives: 14 us -> 0 us
  between operations: 14.4 us -> 0.66 us
    psum x2 -> x0, waiting for transfers between devices: 126 us -> none  [group_psum(): return lax.psum(part_val, 'tp')]
    pallas_call x0 -> x3, Pallas kernels: none -> 116 us  [the longest x1 85 us: run_mlp(): pl.pallas_call(functools.partial(mlp_kernel, chips), out_shape=jax.ShapeD...]
    dot_general x8 -> x0, matrix products: 52.1 us -> none  [the longest x1 25.1 us: layer_steps(): jnp.dot(act, w_down, preferred_element_type=jnp.float32)]
    select_n x1 -> x0, other arithmetic: 17 us -> none  [layer_steps(): jnp.where(offsets == step_idx, new_k[step_idx][:, :, None, :], k_out)]
    psum x1 -> x0, blocking collectives: 14 us -> none  [group_psum(): return lax.psum(part_val, 'tp')]
    convert_element_type x7 -> x0, other arithmetic: 9.44 us -> none  [the longest x1 5.21 us: layer_steps(): (hidden.astype(jnp.float32) + mlp_sum * rms_factor(jnp.sum(mlp_sum * mlp_...]
    reduce_sum x3 -> x0, other arithmetic: 6.11 us -> none  [the longest x1 2.73 us: layer_steps(): jnp.sum(attn_sum * attn_sum, axis=-1, keepdims=True)]
    reshape x1 -> x3, local copies, waits for them, and re-layouts: 0.26 us -> 3.88 us  [the longest x1 1.31 us: run_mlp(): g_mlp.reshape(1, d_model)]
  transfers between devices with their start and end apart: 2 -> 0, of which waited for: 2 -> 0; matrix products, arithmetic and copies ran while one was open for 0% -> 0% of each run, Pallas kernels for 0% -> 0%
where the time goes in v2:
time: 124 us
  Pallas kernels  116 us (94%)
  local copies, waits for them, and re-layouts  7.78 us (6%)
    pallas_call x1, Pallas kernels, run_mlp(): pl.pallas_call(functools.partial(mlp_kernel, chips), out_shape=jax.ShapeD...  85 us
    pallas_call x1, Pallas kernels, run_qkv(): pl.pallas_call(functools.partial(qkv_kernel, tp, width * tp, hd * tp), ou...  16.4 us
    pallas_call x1, Pallas kernels, run_attention(): pl.pallas_call(functools.partial(attention_kernel, steps, heads), out_sha...  14.2 us
    unnamed x1, local copies, waits for them, and re-layouts  3.91 us

profile of v2, /device:TPU:81, one launch (start us, length us, event | category | flops | bytes accessed | tf_op | source)
XLA Modules:
  0.0 124.1 jit_solution(16749352826932775009)
XLA Ops:
  0.6 1.3 %reshape.34.gq_ref = bf16[1,512]{1,0:T(2,128)(2,1)} reshape(bf16[512]{0:T(512)(128)(2,1)} %param.27) | data formatting | bytes 2048 | tf_op jit(solution)/shard_map/reshape | solution.py:139
  1.9 1.3 %reshape.38.ga_ref = bf16[1,4096]{1,0:T(2,128)(2,1)} reshape(bf16[4096]{0:T(1024)(128)(2,1)} %param.29) | data formatting | bytes 16384 | tf_op jit(solution)/shard_map/reshape | solution.py:490
  3.2 1.3 %reshape.39.gm_ref = bf16[1,4096]{1,0:T(2,128)(2,1)} reshape(bf16[4096]{0:T(1024)(128)(2,1)} %param.30) | data formatting | bytes 16384 | tf_op jit(solution)/shard_map/reshape | solution.py:490
  4.5 16.4 %qkv.1 = (bf16[128,16,128]{2,1,0:T(8,128)(2,1)}, f32[3,128,128]{2,1,0:T(8,128)}, f32[3,128,128]{2,1,0:T(8,128)}) custom-call(bf16[3,128,4096]{2,1,0:T(8,128)(2,1)} %x_hbm.3, s32[1,128]{1,0:T(1,128)} %bitcast.12, f32[1,128]{1,0:T(1,128)} %constant.2.clone.freq_ref, bf16[4096,512]{1,0:T(8,128)(2,1)} %wq_hbm.1, bf16[4096,128]{1,0:T(8,128)(2,1)} %wk_hbm.1, ...), custom_call_target="tpu_custom_call" | custom-call | tf_op jit(solution)/shard_map/qkv/pallas_call | solution.py:116
  20.9 14.2 %attention.1 = (bf16[3,128,512]{2,1,0:T(8,128)(2,1)}, bf16[128,256,128]{2,1,0:T(8,128)(2,1)}, bf16[128,256,128]{2,1,0:T(8,128)(2,1)}) custom-call(s32[128]{0:T(128)} %len_ref.1, bf16[128,16,128]{2,1,0:T(8,128)(2,1)} %get-tuple-element.9.q_ref, f32[3,128,128]{2,1,0:T(8,128)} %get-tuple-element.10.kn_ref, f32[3,128,128]{2,1,0:T(8,128)} %get-tuple-element.11.vn_ref, ...), custom_call_target="tpu_custom_call" | custom-call | tf_op jit(solution)/shard_map/attention/pallas_call | solution.py:221
  35.2 85.0 %mlp.1 = bf16[3,128,4096]{2,1,0:T(8,128)(2,1)} custom-call(bf16[3,128,4096]{2,1,0:T(8,128)(2,1)} %x_hbm.3, bf16[3,128,512]{2,1,0:T(8,128)(2,1)} %get-tuple-element.12.o_ref, bf16[512,4096]{1,0:T(8,128)(2,1)} %wo_hbm.1, bf16[4096,1792]{1,0:T(8,128)(2,1)} %w1_hbm.1, bf16[4096,1792]{1,0:T(8,128)(2,1)} %w3_hbm.1, bf16[1792,4096]{1,0:T(8,128)(2,1)} %w2_hbm.1, ...), custom_call_target="tpu_custom_call" | custom-call | tf_op jit(solution)/shard_map/mlp/pallas_call | solution.py:465
  120.2 3.9 %copy.22 = bf16[3,128,4096]{2,1,0:T(8,128)(2,1)} copy(bf16[3,128,4096]{2,1,0:T(8,128)(2,1)} %mlp.1) | data formatting | bytes 6291456

commit v3 on v2

v3 whole, which is shorter than its diff:
```python
import functools

import jax
import jax.numpy as jnp
import numpy as np
from jax import lax
from jax.experimental import pallas as pl
from jax.experimental.pallas import tpu as pltpu
from jax.sharding import PartitionSpec as P

ROPE_THETA = 500000.0
NORM_EPS = 1e-6
F32 = jnp.float32
BF16 = jnp.bfloat16
MESH = pl.DeviceIdType.MESH
VMEM_SPEC = pl.BlockSpec(memory_space=pltpu.VMEM)
ANY_SPEC = pl.BlockSpec(memory_space=pl.ANY)
SMEM_SPEC = pl.BlockSpec(memory_space=pltpu.SMEM)
VMEM_LIMIT = 67043328
SLOT_ROWS = 16


def matmul(lhs, rhs):
    return jnp.dot(lhs, rhs, preferred_element_type=F32)


def qkv_kernel(tp, q_width, kv_width, x_hbm, len_hbm, freq_hbm, wq_hbm, wk_hbm, wv_hbm, gq_hbm, gk_hbm,
               q_hbm, kn_hbm, vn_hbm,
               len_ref, freq_ref, gq_ref, gk_ref, q_out, kn_out, vn_out, small_sem, out_sem, x_buf, wq_buf, wk_buf, wv_buf, q_raw, q_rows, part, inbox, turn, in_sem, send_sem, recv_sem):
    steps, rows, _ = x_hbm.shape
    hd = wk_hbm.shape[1]
    heads = wq_hbm.shape[1] // hd
    pad = q_hbm.shape[1]
    me = lax.axis_index("tp")
    x_in = [pltpu.make_async_copy(x_hbm.at[t], x_buf.at[pl.ds(t * rows, rows), :], in_sem.at[t]) for t in range(steps)]
    for copy in x_in:
        copy.start()
    half = heads * hd // 2
    wk_in = pltpu.make_async_copy(wk_hbm, wk_buf, in_sem.at[3])
    wq_in = [pltpu.make_async_copy(wq_hbm.at[:, pl.ds(j * half, half)], wq_buf.at[:, pl.ds(j * half, half)], in_sem.at[4 + j]) for j in range(2)]
    wv_in = pltpu.make_async_copy(wv_hbm, wv_buf, in_sem.at[6])
    small_in = [pltpu.make_async_copy(src, dst, small_sem.at[i]) for i, (src, dst) in enumerate(
        ((len_hbm, len_ref), (freq_hbm, freq_ref), (gq_hbm, gq_ref), (gk_hbm, gk_ref)))]
    outs = [pltpu.make_async_copy(src, dst, out_sem.at[i]) for i, (src, dst) in enumerate(
        ((q_out, q_hbm), (kn_out, kn_hbm), (vn_out, vn_hbm)))]
    for copy in small_in + [wk_in, wq_in[0], wq_in[1], wv_in]:
        copy.start()

    barrier = pltpu.get_barrier_semaphore()
    for j in range(1, tp):
        pl.semaphore_signal(barrier, inc=1, device_id={"tp": lax.rem(me + j, tp)}, device_id_type=MESH)

    for copy in small_in:
        copy.wait()
    lens = jnp.transpose(jnp.broadcast_to(len_ref[...].astype(F32), (rows, rows)))[:, :hd]
    lane = lax.broadcasted_iota(jnp.int32, (rows, hd), 1)
    sign = jnp.where(lane < hd // 2, -1.0, 1.0).astype(F32)
    tables = []
    for t in range(steps):
        angle = (lens + float(t)) * freq_ref[...]
        tables.append((jnp.cos(angle), jnp.sin(angle) * sign))

    q_rows[...] = jnp.zeros_like(q_rows)
    for copy in x_in:
        copy.wait()
    wk_in.wait()
    k_raw = matmul(x_buf[...], wk_buf[...]).astype(BF16).astype(F32)
    k_sq = jnp.sum(k_raw * k_raw, axis=1, keepdims=True)
    q_sq = None
    for j in range(2):
        wq_in[j].wait()
        val = matmul(x_buf[...], wq_buf[:, j * half:(j + 1) * half]).astype(BF16).astype(F32)
        q_raw[:, j * half:(j + 1) * half] = val
        sq = jnp.sum(val * val, axis=1, keepdims=True)
        q_sq = sq if q_sq is None else q_sq + sq
    packed = jnp.zeros((rows, rows), F32)
    col = lax.broadcasted_iota(jnp.int32, (rows, rows), 1)
    for t in range(steps):
        packed = jnp.where(col == t, q_sq[t * rows:(t + 1) * rows], packed)
        packed = jnp.where(col == steps + t, k_sq[t * rows:(t + 1) * rows], packed)
    part[...] = jnp.transpose(packed)[:part.shape[0]]
    pl.semaphore_wait(barrier, tp - 1)
    copies = []
    for j in range(1, tp):
        copy = pltpu.make_async_remote_copy(
            src_ref=part, dst_ref=inbox.at[j - 1], send_sem=send_sem.at[j - 1], recv_sem=recv_sem.at[j - 1],
            device_id={"tp": lax.rem(me + j, tp)}, device_id_type=MESH)
        copy.start()
        copies.append(copy)
    wv_in.wait()
    vn_out[...] = matmul(x_buf[...], wv_buf[...]).astype(BF16).astype(F32).reshape(steps, rows, hd)
    outs[2].start()
    total = part[...]
    for j in range(1, tp):
        copies[j - 1].wait()
        total = total + inbox[j - 1]
    turn[...] = jnp.zeros_like(turn)
    turn[0:part.shape[0], :] = total
    sums = jnp.transpose(turn[...])
    gain_k = gk_ref[...].astype(F32)
    gain_q = gq_ref[...].astype(F32)
    for t in range(steps):
        cos_tab, sin_tab = tables[t]
        q_fac = lax.rsqrt(sums[:, t:t + 1] / q_width + NORM_EPS)
        k_fac = lax.rsqrt(sums[:, steps + t:steps + t + 1] / kv_width + NORM_EPS)
        val = k_raw[t * rows:(t + 1) * rows] * k_fac * gain_k
        val = val * cos_tab + pltpu.roll(val, hd // 2, axis=1) * sin_tab
        kn_out[t] = val.astype(BF16).astype(F32)
        for g in range(heads):
            val = q_raw[t * rows:(t + 1) * rows, g * hd:(g + 1) * hd] * q_fac * gain_q[g:g + 1, :]
            val = val * cos_tab + pltpu.roll(val, hd // 2, axis=1) * sin_tab
            q_rows[pl.ds(t * heads + g, rows, stride=pad), :] = val
    outs[1].start()
    q_out[...] = q_rows[...].reshape(rows, pad, hd).astype(BF16)
    outs[0].start()
    for copy in outs:
        copy.wait()


def run_qkv(tp, x_seq, cache_len, w_q, w_k, w_v, g_q, g_k):
    steps, rows, d_model = x_seq.shape
    hd = w_k.shape[1]
    width = w_q.shape[1]
    heads = width // hd
    pad = 16
    inv_freq = (ROPE_THETA ** (-(np.arange(hd // 2, dtype=np.float64) * (2.0 / hd)))).astype(np.float32)
    freq = jnp.asarray(np.concatenate([inv_freq, inv_freq])[None, :])
    return pl.pallas_call(
        functools.partial(qkv_kernel, tp, width * tp, hd * tp),
        out_shape=(jax.ShapeDtypeStruct((rows, pad, hd), BF16),
                   jax.ShapeDtypeStruct((steps, rows, hd), F32),
                   jax.ShapeDtypeStruct((steps, rows, hd), F32)),
        in_specs=[ANY_SPEC] * 8,
        out_specs=(ANY_SPEC, ANY_SPEC, ANY_SPEC),
        scratch_shapes=[
            pltpu.VMEM((1, rows), jnp.int32),
            pltpu.VMEM((1, hd), F32),
            pltpu.VMEM((heads, hd), BF16),
            pltpu.VMEM((1, hd), BF16),
            pltpu.VMEM((rows, pad, hd), BF16),
            pltpu.VMEM((steps, rows, hd), F32),
            pltpu.VMEM((steps, rows, hd), F32),
            pltpu.SemaphoreType.DMA((4,)),
            pltpu.SemaphoreType.DMA((3,)),
            pltpu.VMEM((steps * rows, d_model), BF16),
            pltpu.VMEM((d_model, width), BF16),
            pltpu.VMEM((d_model, hd), BF16),
            pltpu.VMEM((d_model, hd), BF16),
            pltpu.VMEM((steps * rows, width), F32),
            pltpu.VMEM((rows * pad, hd), F32),
            pltpu.VMEM((8, rows), F32),
            pltpu.VMEM((tp - 1, 8, rows), F32),
            pltpu.VMEM((rows, rows), F32),
            pltpu.SemaphoreType.DMA((7,)),
            pltpu.SemaphoreType.DMA((tp - 1,)),
            pltpu.SemaphoreType.DMA((tp - 1,)),
        ],
        compiler_params=pltpu.CompilerParams(collective_id=0, has_side_effects=True, vmem_limit_bytes=VMEM_LIMIT),
        name="qkv",
    )(x_seq, cache_len.reshape(1, rows), freq, w_q, w_k, w_v, g_q.reshape(heads, hd), g_k.reshape(1, hd))


SEQ_BLOCK = 8
PATCH_ROWS = 32


def attention_kernel(steps, heads, len_ref, q_hbm, kn_hbm, vn_hbm, k_hbm, v_hbm, o_hbm, k_out, v_out,
                     q_ref, kn_ref, vn_ref, o_ref, small_sem, k_buf, v_buf, mixed, in_sem, out_sem):
    rows, seq_max, hd = k_hbm.shape
    pad = q_hbm.shape[1]
    blocks = rows // SEQ_BLOCK

    def moves(blk, inward):
        sl = pl.ds(blk * SEQ_BLOCK, SEQ_BLOCK)
        if inward:
            return (pltpu.make_async_copy(k_hbm.at[sl], k_buf.at[sl], in_sem.at[0, blk]),
                    pltpu.make_async_copy(v_hbm.at[sl], v_buf.at[sl], in_sem.at[1, blk]))
        return (pltpu.make_async_copy(k_buf.at[sl], k_out.at[sl], out_sem.at[0, blk]),
                pltpu.make_async_copy(v_buf.at[sl], v_out.at[sl], out_sem.at[1, blk]))

    def start_in(blk, carry):
        for copy in moves(blk, True):
            copy.start()
        return carry

    small_in = [pltpu.make_async_copy(src, dst, small_sem.at[i]) for i, (src, dst) in enumerate(
        ((q_hbm, q_ref), (kn_hbm, kn_ref), (vn_hbm, vn_ref)))]
    o_store = pltpu.make_async_copy(o_ref, o_hbm, small_sem.at[3])
    start_in(0, 0)
    for copy in small_in:
        copy.start()
    lax.fori_loop(1, blocks, start_in, 0)
    scale = hd ** -0.5
    win_row = lax.broadcasted_iota(jnp.int32, (PATCH_ROWS, hd), 0)
    key_col = lax.broadcasted_iota(jnp.int32, (pad, seq_max), 1)
    step_row = lax.broadcasted_iota(jnp.int32, (pad, seq_max), 0) // heads
    key_off = key_col - step_row

    def body(blk, carry):
        for copy in moves(blk, True):
            copy.wait()
        lens = []
        for i in range(SEQ_BLOCK):
            b = blk * SEQ_BLOCK + i
            length = len_ref[b]
            base = pl.multiple_of(jnp.minimum((length // 16) * 16, seq_max - PATCH_ROWS), 16)
            for buf, new_ref in ((k_buf, kn_ref), (v_buf, vn_ref)):
                win = buf[b, pl.ds(base, PATCH_ROWS), :].astype(F32)
                for t in range(steps):
                    win = jnp.where(win_row == length + t - base, new_ref[t, pl.ds(b, 1), :], win)
                buf[b, pl.ds(base, PATCH_ROWS), :] = win.astype(BF16)
            lens.append(length)
        scores = []
        for i in range(SEQ_BLOCK):
            b = blk * SEQ_BLOCK + i
            s = lax.dot_general(q_ref[b], k_buf[b], (((1,), (1,)), ((), ())), preferred_element_type=F32) * scale
            scores.append(jnp.where(key_off <= lens[i], s, -jnp.inf))
        exps = []
        for i in range(SEQ_BLOCK):
            e = jnp.exp(scores[i] - jnp.max(scores[i], axis=1, keepdims=True))
            exps.append((e.astype(BF16), jnp.sum(e, axis=1, keepdims=True)))
        for i in range(SEQ_BLOCK):
            b = blk * SEQ_BLOCK + i
            out = matmul(exps[i][0], v_buf[b]) / exps[i][1]
            mixed[pl.ds(pl.multiple_of(b * pad, pad), pad), :] = out
        for copy in moves(blk, False):
            copy.start()
        return carry

    for copy in small_in:
        copy.wait()
    lax.fori_loop(0, blocks, body, 0)
    for t in range(steps):
        for g in range(heads):
            o_ref[t, :, g * hd:(g + 1) * hd] = mixed[pl.ds(t * heads + g, rows, stride=pad), :].astype(BF16)

    o_store.start()

    def finish(blk, carry):
        for copy in moves(blk, False):
            copy.wait()
        return carry

    lax.fori_loop(0, blocks, finish, 0)
    o_store.wait()


def run_attention(heads, cache_len, q_rows, k_new, v_new, k_cache, v_cache):
    rows, _, seq_max, hd = k_cache.shape
    steps = k_new.shape[0]
    pad = q_rows.shape[1]
    flat = jax.ShapeDtypeStruct((rows, seq_max, hd), BF16)
    out, k_out, v_out = pl.pallas_call(
        functools.partial(attention_kernel, steps, heads),
        out_shape=(jax.ShapeDtypeStruct((steps, rows, heads * hd), BF16), flat, flat),
        in_specs=[SMEM_SPEC] + [ANY_SPEC] * 5,
        out_specs=(ANY_SPEC, ANY_SPEC, ANY_SPEC),
        scratch_shapes=[
            pltpu.VMEM(q_rows.shape, BF16),
            pltpu.VMEM(k_new.shape, F32),
            pltpu.VMEM(v_new.shape, F32),
            pltpu.VMEM((steps, rows, heads * hd), BF16),
            pltpu.SemaphoreType.DMA((4,)),
            pltpu.VMEM((rows, seq_max, hd), BF16),
            pltpu.VMEM((rows, seq_max, hd), BF16),
            pltpu.VMEM((rows * pad, hd), F32),
            pltpu.SemaphoreType.DMA((2, rows // SEQ_BLOCK)),
            pltpu.SemaphoreType.DMA((2, rows // SEQ_BLOCK)),
        ],
        compiler_params=pltpu.CompilerParams(vmem_limit_bytes=VMEM_LIMIT),
        name="attention",
    )(cache_len, q_rows, k_new, v_new, k_cache.reshape(rows, seq_max, hd), v_cache.reshape(rows, seq_max, hd))
    return out, k_out.reshape(k_cache.shape), v_out.reshape(v_cache.shape)


QUARTERS = 4
LEFT_PIECES = tuple(range(QUARTERS // 2))
RIGHT_PIECES = tuple(range(QUARTERS // 2, QUARTERS))
PIECED = ("pair", "relay", "near", "far", "own_r", "own_l", "pass")
WHOLE = ("own_s", "sib_r", "sib_l", "sib_fr", "sib_fl")
COPIES = tuple((kind, q) for kind in PIECED for q in range(QUARTERS)) + tuple((kind, 0) for kind in WHOLE)
GATE_TILE = 256
DOWN_TILE = 512
TASKS = ("proj", "pair", "relay", "norm", "pass", "sib", "sibf", "gather", "gate", "down")
ORDER = (
    0, 1, 3, 100, 2, 101, 13, 23, 103, 10, 102, 11, 113, 12, 111, 110, 201, 200, 112, 203, 20, 22, 202, 123,
    120, 210, 213, 212, 122, 21, 211, 300, 121, 400, 402, 403, 401, 310, 501, 220, 221, 223, 500, 600, 601, 222, 700, 410,
    800, 801, 413, 411, 412, 802, 803, 511, 320, 804, 805, 806, 900, 901, 610, 510, 902, 903, 611, 904, 420, 905, 422, 150,
    906, 421, 423, 907, 710, 810, 151, 811, 812, 153, 152, 813, 814, 815, 621, 816, 620, 251, 910, 911, 912, 521, 253, 520,
    913, 250, 914, 252, 160, 915, 916, 917, 720, 820, 161, 821, 822, 163, 823, 350, 260, 162, 824, 825, 826, 920, 921, 922,
    263, 923, 924, 925, 170, 926, 171, 927, 172, 261, 173, 262, 453, 451, 270, 452, 450, 551, 550, 271, 272, 273, 360, 370,
    460, 461, 462, 463, 650, 472, 560, 470, 561, 473, 471, 651, 570, 750, 660, 571, 661, 671, 670, 760, 770,
)


def mlp_kernel(chips, x_hbm, o_hbm, wo_hbm, w1_hbm, w3_hbm, w2_hbm, ga_hbm, gm_hbm, y_out,
               o_ref, ga_ref, gm_ref, small_sem, wo, w1, w3, w2, x_own, gains, part, pair_in, relay_in, near_in, hid, act, w_sem, x_sem, y_sem, send_sem, recv_sem):
    steps, rows, d_model = x_hbm.shape
    ff = w1_hbm.shape[1]
    piece = d_model // QUARTERS
    me = lax.axis_index("tp")
    chip, core = me // 2, lax.rem(me, 2)
    nxt, prv, opp = lax.rem(chip + 1, chips), lax.rem(chip + chips - 1, chips), lax.rem(chip + 2, chips)
    right, left, sib = nxt * 2 + core, prv * 2 + core, chip * 2 + 1 - core
    n_gate, n_down = ff // GATE_TILE, d_model // DOWN_TILE

    def cols(hbm, buf, j, width, sem):
        return pltpu.make_async_copy(hbm.at[:, pl.ds(j * width, width)], buf.at[:, pl.ds(j * width, width)], w_sem.at[sem])

    wo_in = [cols(wo_hbm, wo, j, piece, j) for j in range(QUARTERS)]
    w1_in = [cols(w1_hbm, w1, j, GATE_TILE, QUARTERS + j) for j in range(n_gate)]
    w3_in = [cols(w3_hbm, w3, j, GATE_TILE, QUARTERS + n_gate + j) for j in range(n_gate)]
    w2_in = [cols(w2_hbm, w2, j, DOWN_TILE, QUARTERS + 2 * n_gate + j) for j in range(n_down)]

    def slot(c, k):
        return pl.ds(pl.multiple_of((c * 2 + k) * SLOT_ROWS, SLOT_ROWS), SLOT_ROWS)

    x_in = [pltpu.make_async_copy(x_hbm.at[t, slot(chip, core), :], x_own.at[t], x_sem.at[t]) for t in range(steps)]
    small_in = [pltpu.make_async_copy(src, dst, small_sem.at[i]) for i, (src, dst) in enumerate(
        ((o_hbm, o_ref), (ga_hbm, ga_ref), (gm_hbm, gm_ref)))]
    for copy in small_in + wo_in + x_in:
        copy.start()
    for j in range(n_gate):
        w1_in[j].start()
        w3_in[j].start()
    for copy in w2_in:
        copy.start()

    barrier = pltpu.get_barrier_semaphore()
    for other in (right, left, sib):
        pl.semaphore_signal(barrier, inc=1, device_id={"tp": other}, device_id_type=MESH)
    for copy in small_in:
        copy.wait()
    for i, ref in enumerate((ga_ref, gm_ref)):
        vals = ref[...].astype(F32)
        for j in range(vals.shape[0]):
            gains[i, :, j * vals.shape[1]:(j + 1) * vals.shape[1]] = vals[j:j + 1, :]
    pl.semaphore_wait(barrier, 3)

    def quarter(q, count=1):
        return pl.ds(q * piece, count * piece)

    def endpoints(t, kind, q):
        own, other = part.at[t, :, core], part.at[t, :, 1 - core]
        to_right = q in LEFT_PIECES
        c = quarter(q)
        if kind == "pair":
            return other.at[:, :, c], pair_in.at[t, :, :, c], sib
        if kind == "relay":
            return own.at[opp, :, c], relay_in.at[t, :, c], right if to_right else left
        if kind == "near":
            if to_right:
                return own.at[prv, :, c], near_in.at[t, 1, :, c], left
            return own.at[nxt, :, c], near_in.at[t, 0, :, c], right
        if kind == "far":
            if to_right:
                return own.at[nxt, :, c], near_in.at[t, 0, :, c], right
            return own.at[prv, :, c], near_in.at[t, 1, :, c], left
        if kind == "own_r":
            block, device = hid.at[t, slot(chip, core), c], right
        elif kind == "own_l":
            block, device = hid.at[t, slot(chip, core), c], left
        elif kind == "pass":
            block, device = (hid.at[t, slot(prv, core), c], right) if to_right else (hid.at[t, slot(nxt, core), c], left)
        elif kind == "own_s":
            block, device = hid.at[t, slot(chip, core), :], sib
        elif kind == "sib_r":
            block, device = hid.at[t, slot(prv, core), :], sib
        elif kind == "sib_l":
            block, device = hid.at[t, slot(nxt, core), :], sib
        elif kind == "sib_fr":
            block, device = hid.at[t, slot(opp, core), quarter(0, QUARTERS // 2)], sib
        else:
            block, device = hid.at[t, slot(opp, core), quarter(QUARTERS // 2, QUARTERS // 2)], sib
        return block, block, device

    def copy(ph, t, kind, q=0):
        src, dst, device = endpoints(t, kind, q)
        j = COPIES.index((kind, q))
        return pltpu.make_async_remote_copy(
            src_ref=src, dst_ref=dst, send_sem=send_sem.at[ph, t, j], recv_sem=recv_sem.at[ph, t, j],
            device_id={"tp": device}, device_id_type=MESH)

    def sent(ph, t):
        for kind, q in COPIES:
            copy(ph, t, kind, q).wait_send()

    def proj(ph, t, q):
        if t == 0:
            wo_in[q].wait()
        for n in range(q * piece, (q + 1) * piece, DOWN_TILE):
            val = matmul(o_ref[t], wo[:, n:n + DOWN_TILE]).astype(BF16)
            part[t, :, :, :, n:n + DOWN_TILE] = val.reshape(chips, 2, SLOT_ROWS, DOWN_TILE)
        copy(0, t, "pair", q).start()

    def pair_add(ph, t, q):
        copy(ph, t, "pair", q).wait_recv()
        c = slice(q * piece, (q + 1) * piece)
        for n in (opp, prv, nxt, chip):
            part[t, n, core, :, c] = (part[t, n, core, :, c].astype(F32) + pair_in[t, n, :, c].astype(F32)).astype(BF16)
        copy(ph, t, "relay", q).start()
        copy(ph, t, "near", q).start()

    def relay_add(ph, t, q):
        copy(ph, t, "relay", q).wait_recv()
        c = slice(q * piece, (q + 1) * piece)
        n = nxt if q in LEFT_PIECES else prv
        part[t, n, core, :, c] = (part[t, n, core, :, c].astype(F32) + relay_in[t, :, c].astype(F32)).astype(BF16)
        copy(ph, t, "far", q).start()

    def norm(ph, t, _):
        for q in range(QUARTERS):
            copy(ph, t, "near", q).wait_recv()
            copy(ph, t, "far", q).wait_recv()
        total = part[t, chip, core].astype(F32) + near_in[t, 0].astype(F32) + near_in[t, 1].astype(F32)
        total = total.astype(BF16).astype(F32)
        fac = lax.rsqrt(jnp.sum(total * total, axis=1, keepdims=True) / d_model + NORM_EPS)
        if ph == 0:
            x_in[t].wait()
            base = x_own[t]
        else:
            base = hid[t, slot(chip, core), :]
        hid[t, slot(chip, core), :] = (base.astype(F32) + total * fac * gains[ph]).astype(BF16)
        for first, second in ((LEFT_PIECES, RIGHT_PIECES), (RIGHT_PIECES, LEFT_PIECES)):
            for i, j in zip(first, second):
                copy(ph, t, "own_r", i).start()
                copy(ph, t, "own_l", j).start()
        copy(ph, t, "own_s").start()

    def pass_on(ph, t, q):
        copy(ph, t, "own_r" if q in LEFT_PIECES else "own_l", q).wait_recv()
        copy(ph, t, "pass", q).start()

    def pass_sib(ph, t, side):
        for q in (RIGHT_PIECES, LEFT_PIECES)[side]:
            copy(ph, t, ("own_r", "own_l")[side], q).wait_recv()
        copy(ph, t, ("sib_r", "sib_l")[side]).start()

    def far_sib(ph, t, side):
        for q in (LEFT_PIECES, RIGHT_PIECES)[side]:
            copy(ph, t, "pass", q).wait_recv()
        copy(ph, t, ("sib_fr", "sib_fl")[side]).start()

    def gather(ph, t, _):
        for kind in WHOLE:
            copy(ph, t, kind).wait_recv()
        if ph == 1:
            pltpu.make_async_copy(hid.at[t], y_out.at[t], y_sem.at[t]).start()

    def gate_up(ph, t, j):
        if t == 0:
            w1_in[j].wait()
            w3_in[j].wait()
        sl = slice(j * GATE_TILE, (j + 1) * GATE_TILE)
        gate = matmul(hid[t], w1[:, sl])
        up = matmul(hid[t], w3[:, sl])
        act[:, sl] = (gate / (1.0 + jnp.exp(-gate)) * up).astype(BF16)

    def down(ph, t, j):
        if j == 0:
            sent(0, t)
        if t == 0:
            w2_in[j].wait()
        sl = slice(j * DOWN_TILE, (j + 1) * DOWN_TILE)
        val = matmul(act[...], w2[:, sl]).astype(BF16)
        part[t, :, :, :, sl] = val.reshape(chips, 2, SLOT_ROWS, DOWN_TILE)
        if (j + 1) * DOWN_TILE % piece == 0:
            copy(1, t, "pair", (j + 1) * DOWN_TILE // piece - 1).start()

    run = (proj, pair_add, relay_add, norm, pass_on, pass_sib, far_sib, gather, gate_up, down)
    for code in ORDER:
        run[code // 100](code // 50 % 2, code % 50 // 10, code % 10)
    for t in range(steps):
        sent(1, t)
        pltpu.make_async_copy(hid.at[t], y_out.at[t], y_sem.at[t]).wait()


def run_mlp(tp, x_seq, attn, w_o, w_gate, w_up, w_down, g_attn, g_mlp):
    steps, rows, d_model = x_seq.shape
    ff = w_gate.shape[1]
    chips = tp // 2
    n_sem = QUARTERS + 2 * (ff // GATE_TILE) + d_model // DOWN_TILE
    return pl.pallas_call(
        functools.partial(mlp_kernel, chips),
        out_shape=jax.ShapeDtypeStruct((steps, rows, d_model), BF16),
        in_specs=[ANY_SPEC] * 8,
        out_specs=ANY_SPEC,
        scratch_shapes=[
            pltpu.VMEM(attn.shape, BF16),
            pltpu.VMEM((d_model // 128, 128), BF16),
            pltpu.VMEM((d_model // 128, 128), BF16),
            pltpu.SemaphoreType.DMA((3,)),
            pltpu.VMEM(w_o.shape, BF16),
            pltpu.VMEM(w_gate.shape, BF16),
            pltpu.VMEM(w_up.shape, BF16),
            pltpu.VMEM(w_down.shape, BF16),
            pltpu.VMEM((steps, SLOT_ROWS, d_model), BF16),
            pltpu.VMEM((2, 1, d_model), F32),
            pltpu.VMEM((steps, chips, 2, SLOT_ROWS, d_model), BF16),
            pltpu.VMEM((steps, chips, SLOT_ROWS, d_model), BF16),
            pltpu.VMEM((steps, SLOT_ROWS, d_model), BF16),
            pltpu.VMEM((steps, 2, SLOT_ROWS, d_model), BF16),
            pltpu.VMEM((steps, rows, d_model), BF16),
            pltpu.VMEM((rows, ff), BF16),
            pltpu.SemaphoreType.DMA((n_sem,)),
            pltpu.SemaphoreType.DMA((steps,)),
            pltpu.SemaphoreType.DMA((steps,)),
            pltpu.SemaphoreType.DMA((2, steps, len(COPIES))),
            pltpu.SemaphoreType.DMA((2, steps, len(COPIES))),
        ],
        compiler_params=pltpu.CompilerParams(collective_id=1, has_side_effects=True, vmem_limit_bytes=VMEM_LIMIT),
        name="mlp",
    )(x_seq, attn, w_o, w_gate, w_up, w_down, g_attn.reshape(-1, 128), g_mlp.reshape(-1, 128))


COPY_ROWS = 64


def store_kernel(src, dst, buf, in_sem, out_sem):
    rows = src.shape[0]
    n = rows // COPY_ROWS
    sl = [pl.ds(i * COPY_ROWS, COPY_ROWS) for i in range(n)]
    ins = [pltpu.make_async_copy(src.at[sl[i]], buf.at[sl[i]], in_sem.at[i]) for i in range(n)]
    outs = [pltpu.make_async_copy(buf.at[sl[i]], dst.at[sl[i]], out_sem.at[i]) for i in range(n)]
    for i in range(n):
        ins[i].start()
    for i in range(n):
        ins[i].wait()
        outs[i].start()
    for i in range(n):
        outs[i].wait()


def run_store(y_seq):
    steps, rows, d_model = y_seq.shape
    total = steps * rows
    return pl.pallas_call(
        store_kernel,
        out_shape=jax.ShapeDtypeStruct((total, d_model), BF16),
        in_specs=[ANY_SPEC],
        out_specs=ANY_SPEC,
        scratch_shapes=[
            pltpu.VMEM((total, d_model), BF16),
            pltpu.SemaphoreType.DMA((total // COPY_ROWS,)),
            pltpu.SemaphoreType.DMA((total // COPY_ROWS,)),
        ],
        compiler_params=pltpu.CompilerParams(vmem_limit_bytes=VMEM_LIMIT),
        name="store",
    )(y_seq.reshape(total, d_model)).reshape(y_seq.shape)


def solution(mesh):
    tp = mesh.shape['tp']

    def local_run(x_seq, cache_len, k_cache, v_cache, w_q, w_k, w_v, w_o, w_gate, w_up, w_down, g_q, g_k, g_attn, g_mlp):
        heads = w_q.shape[1] // w_k.shape[1]
        q_rows, k_new, v_new = run_qkv(tp, x_seq, cache_len, w_q, w_k, w_v, g_q, g_k)
        attn, k_out, v_out = run_attention(heads, cache_len, q_rows, k_new, v_new, k_cache, v_cache)
        y_seq = run_mlp(tp, x_seq, attn, w_o, w_gate, w_up, w_down, g_attn, g_mlp)
        return run_store(y_seq), k_out, v_out

    data_spec = P(None, 'dp', None)
    cache_spec = P('dp', 'tp', None, None)
    col_spec = P(None, 'tp')
    row_spec = P('tp', None)
    arg_specs = (data_spec, P('dp'), cache_spec, cache_spec, col_spec, col_spec, col_spec, row_spec, col_spec, col_spec, row_spec, P('tp'), P('tp'), P(None), P(None))
    out_specs = (data_spec, cache_spec, cache_spec)
    return jax.shard_map(local_run, mesh=mesh, in_specs=arg_specs, out_specs=out_specs, check_vma=False)
```

time: 124 us -> 119 us (0.960)
  local copies, waits for them, and re-layouts: 7.78 us -> 0 us
  Pallas kernels: 116 us -> 118 us
    unnamed x1 -> x0, local copies, waits for them, and re-layouts: 3.91 us -> none
    reshape x3 -> x0, local copies, waits for them, and re-layouts: 3.88 us -> none  [the longest x1 1.31 us: run_mlp(): g_mlp.reshape(1, d_model)]
    pallas_call x0 -> x1, Pallas kernels: none -> 2.8 us  [run_store(): pl.pallas_call(store_kernel, out_shape=jax.ShapeDtypeStruct((total, d_mod...]
where the time goes in v3:
time: 119 us
  Pallas kernels  118 us (99%)
    pallas_call x1, Pallas kernels, run_mlp(): pl.pallas_call(functools.partial(mlp_kernel, chips), out_shape=jax.ShapeD...  84.6 us
    pallas_call x1, Pallas kernels, run_qkv(): pl.pallas_call(functools.partial(qkv_kernel, tp, width * tp, hd * tp), ou...  17.6 us
    pallas_call x1, Pallas kernels, run_attention(): pl.pallas_call(functools.partial(attention_kernel, steps, heads), out_sha...  13.5 us
    pallas_call x1, Pallas kernels, run_store(): pl.pallas_call(store_kernel, out_shape=jax.ShapeDtypeStruct((total, d_mod...  2.8 us

profile of v3, /device:TPU:81, one launch (start us, length us, event | category | flops | bytes accessed | tf_op | source)
XLA Modules:
  0.0 119.4 jit_solution(10965313002272730865)
XLA Ops:
  0.6 17.6 %qkv.1 = (bf16[128,16,128]{2,1,0:T(8,128)(2,1)}, f32[3,128,128]{2,1,0:T(8,128)}, f32[3,128,128]{2,1,0:T(8,128)}) custom-call(bf16[3,128,4096]{2,1,0:T(8,128)(2,1)} %x_hbm.3, s32[1,128]{1,0:T(1,128)} %bitcast.21, f32[1,128]{1,0:T(1,128)} %constant.2.clone.freq_hbm, bf16[4096,512]{1,0:T(8,128)(2,1)} %wq_hbm.1, bf16[4096,128]{1,0:T(8,128)(2,1)} %wk_hbm.1, ...), custom_call_target="tpu_custom_call" | custom-call | tf_op jit(solution)/shard_map/qkv/pallas_call | solution.py:128
  18.2 13.5 %attention.1 = (bf16[3,128,512]{2,1,0:T(8,128)(2,1)}, bf16[128,256,128]{2,1,0:T(8,128)(2,1)}, bf16[128,256,128]{2,1,0:T(8,128)(2,1)}) custom-call(s32[128]{0:T(128)} %len_ref.1, bf16[128,16,128]{2,1,0:T(8,128)(2,1)} %get-tuple-element.9.q_hbm, f32[3,128,128]{2,1,0:T(8,128)} %get-tuple-element.10.kn_hbm, f32[3,128,128]{2,1,0:T(8,128)} %get-tuple-element.11.vn_hbm, ...), custom_call_target="tpu_custom_call" | custom-call | tf_op jit(solution)/shard_map/attention/pallas_call | solution.py:253
  31.8 84.6 %mlp.1 = bf16[3,128,4096]{2,1,0:T(8,128)(2,1)} custom-call(bf16[3,128,4096]{2,1,0:T(8,128)(2,1)} %x_hbm.3, bf16[3,128,512]{2,1,0:T(8,128)(2,1)} %get-tuple-element.12.o_hbm, bf16[512,4096]{1,0:T(8,128)(2,1)} %wo_hbm.1, bf16[4096,1792]{1,0:T(8,128)(2,1)} %w1_hbm.1, bf16[4096,1792]{1,0:T(8,128)(2,1)} %w3_hbm.1, bf16[1792,4096]{1,0:T(8,128)(2,1)} %w2_hbm.1, ...), custom_call_target="tpu_custom_call" | custom-call | tf_op jit(solution)/shard_map/mlp/pallas_call | solution.py:483
  116.4 2.8 %store.1 = bf16[384,4096]{1,0:T(8,128)(2,1)} custom-call(bf16[384,4096]{1,0:T(8,128)(2,1)} %bitcast.15), custom_call_target="tpu_custom_call" | custom-call | tf_op jit(solution)/shard_map/store/pallas_call | solution.py:537

commit v4 on v3

--- a/solution.py
+++ b/solution.py
@@ -320,11 +320,7 @@
         ((o_hbm, o_ref), (ga_hbm, ga_ref), (gm_hbm, gm_ref)))]
     for copy in small_in + wo_in + x_in:
         copy.start()
-    for j in range(n_gate):
-        w1_in[j].start()
-        w3_in[j].start()
-    for copy in w2_in:
-        copy.start()
+    later = [copy for pair in zip(w1_in, w3_in) for copy in pair] + w2_in
 
     barrier = pltpu.get_barrier_semaphore()
     for other in (right, left, sib):
@@ -468,8 +464,13 @@
             copy(1, t, "pair", (j + 1) * DOWN_TILE // piece - 1).start()
 
     run = (proj, pair_add, relay_add, norm, pass_on, pass_sib, far_sib, gather, gate_up, down)
+    gates_from = TASKS.index("gate") * 100
     for code in ORDER:
+        while later and code >= gates_from and (len(later) > n_down or later[0] is w2_in[0]):
+            later.pop(0).start()
         run[code // 100](code // 50 % 2, code % 50 // 10, code % 10)
+        if later:
+            later.pop(0).start()
     for t in range(steps):
         sent(1, t)
         pltpu.make_async_copy(hid.at[t], y_out.at[t], y_sem.at[t]).wait()

time: 119 us -> 107 us (0.90)
  Pallas kernels: 118 us -> 106 us
    pallas_call x1, Pallas kernels: 84.6 us -> 71.9 us  [run_mlp(): pl.pallas_call(functools.partial(mlp_kernel, chips), out_shape=jax.ShapeD...]
where the time goes in v4:
time: 107 us
  Pallas kernels  106 us (99%)
    pallas_call x1, Pallas kernels, run_mlp(): pl.pallas_call(functools.partial(mlp_kernel, chips), out_shape=jax.ShapeD...  71.9 us
    pallas_call x1, Pallas kernels, run_qkv(): pl.pallas_call(functools.partial(qkv_kernel, tp, width * tp, hd * tp), ou...  17.6 us
    pallas_call x1, Pallas kernels, run_attention(): pl.pallas_call(functools.partial(attention_kernel, steps, heads), out_sha...  13.5 us
    pallas_call x1, Pallas kernels, run_store(): pl.pallas_call(store_kernel, out_shape=jax.ShapeDtypeStruct((total, d_mod...  2.8 us

profile of v4, /device:TPU:81, one launch (start us, length us, event | category | flops | bytes accessed | tf_op | source)
XLA Modules:
  0.0 106.7 jit_solution(5965614977456863555)
XLA Ops:
  0.6 17.6 %qkv.1 = (bf16[128,16,128]{2,1,0:T(8,128)(2,1)}, f32[3,128,128]{2,1,0:T(8,128)}, f32[3,128,128]{2,1,0:T(8,128)}) custom-call(bf16[3,128,4096]{2,1,0:T(8,128)(2,1)} %x_hbm.3, s32[1,128]{1,0:T(1,128)} %bitcast.21, f32[1,128]{1,0:T(1,128)} %constant.2.clone.freq_hbm, bf16[4096,512]{1,0:T(8,128)(2,1)} %wq_hbm.1, bf16[4096,128]{1,0:T(8,128)(2,1)} %wk_hbm.1, ...), custom_call_target="tpu_custom_call" | custom-call | tf_op jit(solution)/shard_map/qkv/pallas_call | solution.py:128
  18.2 13.5 %attention.1 = (bf16[3,128,512]{2,1,0:T(8,128)(2,1)}, bf16[128,256,128]{2,1,0:T(8,128)(2,1)}, bf16[128,256,128]{2,1,0:T(8,128)(2,1)}) custom-call(s32[128]{0:T(128)} %len_ref.1, bf16[128,16,128]{2,1,0:T(8,128)(2,1)} %get-tuple-element.9.q_hbm, f32[3,128,128]{2,1,0:T(8,128)} %get-tuple-element.10.kn_hbm, f32[3,128,128]{2,1,0:T(8,128)} %get-tuple-element.11.vn_hbm, ...), custom_call_target="tpu_custom_call" | custom-call | tf_op jit(solution)/shard_map/attention/pallas_call | solution.py:253
  31.8 71.9 %mlp.1 = bf16[3,128,4096]{2,1,0:T(8,128)(2,1)} custom-call(bf16[3,128,4096]{2,1,0:T(8,128)(2,1)} %x_hbm.3, bf16[3,128,512]{2,1,0:T(8,128)(2,1)} %get-tuple-element.12.o_hbm, bf16[512,4096]{1,0:T(8,128)(2,1)} %wo_hbm.1, bf16[4096,1792]{1,0:T(8,128)(2,1)} %w1_hbm.1, bf16[4096,1792]{1,0:T(8,128)(2,1)} %w3_hbm.1, bf16[1792,4096]{1,0:T(8,128)(2,1)} %w2_hbm.1, ...), custom_call_target="tpu_custom_call" | custom-call | tf_op jit(solution)/shard_map/mlp/pallas_call | solution.py:484
  103.7 2.8 %store.1 = bf16[384,4096]{1,0:T(8,128)(2,1)} custom-call(bf16[384,4096]{1,0:T(8,128)(2,1)} %bitcast.15), custom_call_target="tpu_custom_call" | custom-call | tf_op jit(solution)/shard_map/store/pallas_call | solution.py:538

commit v5 on v3

--- a/solution.py
+++ b/solution.py
@@ -16,21 +16,30 @@
 VMEM_SPEC = pl.BlockSpec(memory_space=pltpu.VMEM)
 ANY_SPEC = pl.BlockSpec(memory_space=pl.ANY)
 SMEM_SPEC = pl.BlockSpec(memory_space=pltpu.SMEM)
-VMEM_LIMIT = 67043328
+QKV_VMEM = 40 * 1024 * 1024
+ATTENTION_VMEM = 24 * 1024 * 1024
+MLP_VMEM = 54 * 1024 * 1024
 SLOT_ROWS = 16
+
+
+def in_vmem(val):
+    return pltpu.with_memory_space_constraint(val, pltpu.VMEM)
 
 
 def matmul(lhs, rhs):
     return jnp.dot(lhs, rhs, preferred_element_type=F32)
 
 
-def qkv_kernel(tp, q_width, kv_width, x_hbm, len_hbm, freq_hbm, wq_hbm, wk_hbm, wv_hbm, gq_hbm, gk_hbm,
-               q_hbm, kn_hbm, vn_hbm,
-               len_ref, freq_ref, gq_ref, gk_ref, q_out, kn_out, vn_out, small_sem, out_sem, x_buf, wq_buf, wk_buf, wv_buf, q_raw, q_rows, part, inbox, turn, in_sem, send_sem, recv_sem):
+CACHE_PARTS = 4
+
+
+def qkv_kernel(tp, q_width, kv_width, x_hbm, len_hbm, freq_hbm, wq_hbm, wk_hbm, wv_hbm, gq_hbm, gk_hbm, kc_hbm, vc_hbm,
+               q_out, kn_out, vn_out, kc_out, vc_out,
+               len_ref, freq_ref, gq_ref, gk_ref, small_sem, cache_sem, x_buf, wq_buf, wk_buf, wv_buf, q_raw, q_rows, part, inbox, turn, in_sem, send_sem, recv_sem):
     steps, rows, _ = x_hbm.shape
     hd = wk_hbm.shape[1]
     heads = wq_hbm.shape[1] // hd
-    pad = q_hbm.shape[1]
+    pad = q_out.shape[1]
     me = lax.axis_index("tp")
     x_in = [pltpu.make_async_copy(x_hbm.at[t], x_buf.at[pl.ds(t * rows, rows), :], in_sem.at[t]) for t in range(steps)]
     for copy in x_in:
@@ -41,8 +50,9 @@
     wv_in = pltpu.make_async_copy(wv_hbm, wv_buf, in_sem.at[6])
     small_in = [pltpu.make_async_copy(src, dst, small_sem.at[i]) for i, (src, dst) in enumerate(
         ((len_hbm, len_ref), (freq_hbm, freq_ref), (gq_hbm, gq_ref), (gk_hbm, gk_ref)))]
-    outs = [pltpu.make_async_copy(src, dst, out_sem.at[i]) for i, (src, dst) in enumerate(
-        ((q_out, q_hbm), (kn_out, kn_hbm), (vn_out, vn_hbm)))]
+    seqs = rows // CACHE_PARTS
+    cache_in = [pltpu.make_async_copy(src.at[pl.ds(i * seqs, seqs)], dst.at[pl.ds(i * seqs, seqs)], cache_sem.at[c, i])
+                for i in range(CACHE_PARTS) for c, (src, dst) in enumerate(((kc_hbm, kc_out), (vc_hbm, vc_out)))]
     for copy in small_in + [wk_in, wq_in[0], wq_in[1], wv_in]:
         copy.start()
 
@@ -69,6 +79,8 @@
     q_sq = None
     for j in range(2):
         wq_in[j].wait()
+        if j == 1:
+            cache_in[0].start()
         val = matmul(x_buf[...], wq_buf[:, j * half:(j + 1) * half]).astype(BF16).astype(F32)
         q_raw[:, j * half:(j + 1) * half] = val
         sq = jnp.sum(val * val, axis=1, keepdims=True)
@@ -87,9 +99,10 @@
             device_id={"tp": lax.rem(me + j, tp)}, device_id_type=MESH)
         copy.start()
         copies.append(copy)
+    for copy in cache_in[1:]:
+        copy.start()
     wv_in.wait()
     vn_out[...] = matmul(x_buf[...], wv_buf[...]).astype(BF16).astype(F32).reshape(steps, rows, hd)
-    outs[2].start()
     total = part[...]
     for j in range(1, tp):
         copies[j - 1].wait()
@@ -110,14 +123,12 @@
             val = q_raw[t * rows:(t + 1) * rows, g * hd:(g + 1) * hd] * q_fac * gain_q[g:g + 1, :]
             val = val * cos_tab + pltpu.roll(val, hd // 2, axis=1) * sin_tab
             q_rows[pl.ds(t * heads + g, rows, stride=pad), :] = val
-    outs[1].start()
     q_out[...] = q_rows[...].reshape(rows, pad, hd).astype(BF16)
-    outs[0].start()
-    for copy in outs:
+    for copy in cache_in:
         copy.wait()
 
 
-def run_qkv(tp, x_seq, cache_len, w_q, w_k, w_v, g_q, g_k):
+def run_qkv(tp, x_seq, cache_len, w_q, w_k, w_v, g_q, g_k, k_cache, v_cache):
     steps, rows, d_model = x_seq.shape
     hd = w_k.shape[1]
     width = w_q.shape[1]
@@ -127,21 +138,20 @@
     freq = jnp.asarray(np.concatenate([inv_freq, inv_freq])[None, :])
     return pl.pallas_call(
         functools.partial(qkv_kernel, tp, width * tp, hd * tp),
-        out_shape=(jax.ShapeDtypeStruct((rows, pad, hd), BF16),
-                   jax.ShapeDtypeStruct((steps, rows, hd), F32),
-                   jax.ShapeDtypeStruct((steps, rows, hd), F32)),
-        in_specs=[ANY_SPEC] * 8,
-        out_specs=(ANY_SPEC, ANY_SPEC, ANY_SPEC),
+        out_shape=(pltpu.VMEM((rows, pad, hd), BF16),
+                   pltpu.VMEM((steps, rows, hd), F32),
+                   pltpu.VMEM((steps, rows, hd), F32),
+                   pltpu.VMEM(k_cache.shape, BF16),
+                   pltpu.VMEM(v_cache.shape, BF16)),
+        in_specs=[ANY_SPEC] * 10,
+        out_specs=(VMEM_SPEC,) * 5,
         scratch_shapes=[
             pltpu.VMEM((1, rows), jnp.int32),
             pltpu.VMEM((1, hd), F32),
             pltpu.VMEM((heads, hd), BF16),
             pltpu.VMEM((1, hd), BF16),
-            pltpu.VMEM((rows, pad, hd), BF16),
-            pltpu.VMEM((steps, rows, hd), F32),
-            pltpu.VMEM((steps, rows, hd), F32),
             pltpu.SemaphoreType.DMA((4,)),
-            pltpu.SemaphoreType.DMA((3,)),
+            pltpu.SemaphoreType.DMA((2, CACHE_PARTS)),
             pltpu.VMEM((steps * rows, d_model), BF16),
             pltpu.VMEM((d_model, width), BF16),
             pltpu.VMEM((d_model, hd), BF16),
@@ -155,41 +165,29 @@
             pltpu.SemaphoreType.DMA((tp - 1,)),
             pltpu.SemaphoreType.DMA((tp - 1,)),
         ],
-        compiler_params=pltpu.CompilerParams(collective_id=0, has_side_effects=True, vmem_limit_bytes=VMEM_LIMIT),
+        compiler_params=pltpu.CompilerParams(collective_id=0, has_side_effects=True, vmem_limit_bytes=QKV_VMEM),
         name="qkv",
-    )(x_seq, cache_len.reshape(1, rows), freq, w_q, w_k, w_v, g_q.reshape(heads, hd), g_k.reshape(1, hd))
+    )(x_seq, cache_len.reshape(1, rows), freq, w_q, w_k, w_v, g_q.reshape(heads, hd), g_k.reshape(1, hd), k_cache, v_cache)
 
 
 SEQ_BLOCK = 8
 PATCH_ROWS = 32
 
 
-def attention_kernel(steps, heads, len_ref, q_hbm, kn_hbm, vn_hbm, k_hbm, v_hbm, o_hbm, k_out, v_out,
-                     q_ref, kn_ref, vn_ref, o_ref, small_sem, k_buf, v_buf, mixed, in_sem, out_sem):
-    rows, seq_max, hd = k_hbm.shape
-    pad = q_hbm.shape[1]
+def attention_kernel(steps, heads, len_ref, q_ref, kn_ref, vn_ref, k_in, v_in, wo_hbm, k_out, v_out, k_buf, v_buf, part,
+                     o_ref, wo, mixed, wo_sem, out_sem):
+    rows, seq_max, hd = k_buf.shape
+    pad = q_ref.shape[1]
     blocks = rows // SEQ_BLOCK
-
-    def moves(blk, inward):
+    d_model = wo.shape[1]
+    wo_in = pltpu.make_async_copy(wo_hbm, wo, wo_sem)
+    wo_in.start()
+
+    def moves(blk):
         sl = pl.ds(blk * SEQ_BLOCK, SEQ_BLOCK)
-        if inward:
-            return (pltpu.make_async_copy(k_hbm.at[sl], k_buf.at[sl], in_sem.at[0, blk]),
-                    pltpu.make_async_copy(v_hbm.at[sl], v_buf.at[sl], in_sem.at[1, blk]))
         return (pltpu.make_async_copy(k_buf.at[sl], k_out.at[sl], out_sem.at[0, blk]),
                 pltpu.make_async_copy(v_buf.at[sl], v_out.at[sl], out_sem.at[1, blk]))
 
-    def start_in(blk, carry):
-        for copy in moves(blk, True):
-            copy.start()
-        return carry
-
-    small_in = [pltpu.make_async_copy(src, dst, small_sem.at[i]) for i, (src, dst) in enumerate(
-        ((q_hbm, q_ref), (kn_hbm, kn_ref), (vn_hbm, vn_ref)))]
-    o_store = pltpu.make_async_copy(o_ref, o_hbm, small_sem.at[3])
-    start_in(0, 0)
-    for copy in small_in:
-        copy.start()
-    lax.fori_loop(1, blocks, start_in, 0)
     scale = hd ** -0.5
     win_row = lax.broadcasted_iota(jnp.int32, (PATCH_ROWS, hd), 0)
     key_col = lax.broadcasted_iota(jnp.int32, (pad, seq_max), 1)
@@ -197,8 +195,6 @@
     key_off = key_col - step_row
 
     def body(blk, carry):
-        for copy in moves(blk, True):
-            copy.wait()
         lens = []
         for i in range(SEQ_BLOCK):
             b = blk * SEQ_BLOCK + i
@@ -223,54 +219,52 @@
             b = blk * SEQ_BLOCK + i
             out = matmul(exps[i][0], v_buf[b]) / exps[i][1]
             mixed[pl.ds(pl.multiple_of(b * pad, pad), pad), :] = out
-        for copy in moves(blk, False):
+        for copy in moves(blk):
             copy.start()
         return carry
 
-    for copy in small_in:
-        copy.wait()
     lax.fori_loop(0, blocks, body, 0)
     for t in range(steps):
         for g in range(heads):
-            o_ref[t, :, g * hd:(g + 1) * hd] = mixed[pl.ds(t * heads + g, rows, stride=pad), :].astype(BF16)
-
-    o_store.start()
+            o_ref[t * rows:(t + 1) * rows, g * hd:(g + 1) * hd] = mixed[pl.ds(t * heads + g, rows, stride=pad), :].astype(BF16)
+
+    wo_in.wait()
+    for n in range(0, d_model, DOWN_TILE):
+        val = matmul(o_ref[...], wo[:, n:n + DOWN_TILE]).astype(BF16)
+        part[:, :, :, :, n:n + DOWN_TILE] = val.reshape(part.shape[:4] + (DOWN_TILE,))
 
     def finish(blk, carry):
-        for copy in moves(blk, False):
+        for copy in moves(blk):
             copy.wait()
         return carry
 
     lax.fori_loop(0, blocks, finish, 0)
-    o_store.wait()
-
-
-def run_attention(heads, cache_len, q_rows, k_new, v_new, k_cache, v_cache):
-    rows, _, seq_max, hd = k_cache.shape
+
+
+def run_attention(tp, heads, cache_len, q_rows, k_new, v_new, k_cache, v_cache, w_o):
+    rows, seq_max, hd = k_cache.shape
     steps = k_new.shape[0]
     pad = q_rows.shape[1]
-    flat = jax.ShapeDtypeStruct((rows, seq_max, hd), BF16)
-    out, k_out, v_out = pl.pallas_call(
+    flat = jax.ShapeDtypeStruct(k_cache.shape, BF16)
+    held = pltpu.VMEM(k_cache.shape, BF16)
+    part = pltpu.VMEM((steps, tp // 2, 2, rows // tp, w_o.shape[1]), BF16)
+    k_out, v_out, _, _, part = pl.pallas_call(
         functools.partial(attention_kernel, steps, heads),
-        out_shape=(jax.ShapeDtypeStruct((steps, rows, heads * hd), BF16), flat, flat),
-        in_specs=[SMEM_SPEC] + [ANY_SPEC] * 5,
-        out_specs=(ANY_SPEC, ANY_SPEC, ANY_SPEC),
+        out_shape=(flat, flat, held, held, part),
+        in_specs=[SMEM_SPEC] + [VMEM_SPEC] * 5 + [ANY_SPEC],
+        out_specs=(ANY_SPEC, ANY_SPEC, VMEM_SPEC, VMEM_SPEC, VMEM_SPEC),
+        input_output_aliases={4: 2, 5: 3},
         scratch_shapes=[
-            pltpu.VMEM(q_rows.shape, BF16),
-            pltpu.VMEM(k_new.shape, F32),
-            pltpu.VMEM(v_new.shape, F32),
-            pltpu.VMEM((steps, rows, heads * hd), BF16),
-            pltpu.SemaphoreType.DMA((4,)),
-            pltpu.VMEM((rows, seq_max, hd), BF16),
-            pltpu.VMEM((rows, seq_max, hd), BF16),
+            pltpu.VMEM((steps * rows, heads * hd), BF16),
+            pltpu.VMEM(w_o.shape, BF16),
             pltpu.VMEM((rows * pad, hd), F32),
-            pltpu.SemaphoreType.DMA((2, rows // SEQ_BLOCK)),
+            pltpu.SemaphoreType.DMA,
             pltpu.SemaphoreType.DMA((2, rows // SEQ_BLOCK)),
         ],
-        compiler_params=pltpu.CompilerParams(vmem_limit_bytes=VMEM_LIMIT),
+        compiler_params=pltpu.CompilerParams(vmem_limit_bytes=ATTENTION_VMEM),
         name="attention",
-    )(cache_len, q_rows, k_new, v_new, k_cache.reshape(rows, seq_max, hd), v_cache.reshape(rows, seq_max, hd))
-    return out, k_out.reshape(k_cache.shape), v_out.reshape(v_cache.shape)
+    )(cache_len, in_vmem(q_rows), in_vmem(k_new), in_vmem(v_new), in_vmem(k_cache), in_vmem(v_cache), w_o)
+    return part, k_out, v_out
 
 
 QUARTERS = 4
@@ -280,21 +274,23 @@
 WHOLE = ("own_s", "sib_r", "sib_l", "sib_fr", "sib_fl")
 COPIES = tuple((kind, q) for kind in PIECED for q in range(QUARTERS)) + tuple((kind, 0) for kind in WHOLE)
 GATE_TILE = 256
+FETCHES = 1
 DOWN_TILE = 512
-TASKS = ("proj", "pair", "relay", "norm", "pass", "sib", "sibf", "gather", "gate", "down")
+TASKS = ("send", "pair", "relay", "norm", "pass", "sib", "sibf", "gather", "gate", "down", "fetch")
 ORDER = (
-    0, 1, 3, 100, 2, 101, 13, 23, 103, 10, 102, 11, 113, 12, 111, 110, 201, 200, 112, 203, 20, 22, 202, 123,
-    120, 210, 213, 212, 122, 21, 211, 300, 121, 400, 402, 403, 401, 310, 501, 220, 221, 223, 500, 600, 601, 222, 700, 410,
-    800, 801, 413, 411, 412, 802, 803, 511, 320, 804, 805, 806, 900, 901, 610, 510, 902, 903, 611, 904, 420, 905, 422, 150,
-    906, 421, 423, 907, 710, 810, 151, 811, 812, 153, 152, 813, 814, 815, 621, 816, 620, 251, 910, 911, 912, 521, 253, 520,
-    913, 250, 914, 252, 160, 915, 916, 917, 720, 820, 161, 821, 822, 163, 823, 350, 260, 162, 824, 825, 826, 920, 921, 922,
-    263, 923, 924, 925, 170, 926, 171, 927, 172, 261, 173, 262, 453, 451, 270, 452, 450, 551, 550, 271, 272, 273, 360, 370,
-    460, 461, 462, 463, 650, 472, 560, 470, 561, 473, 471, 651, 570, 750, 660, 571, 661, 671, 670, 760, 770,
+    0, 1000, 1, 1001, 3, 1010, 100, 1011, 2, 1020, 101, 1021, 13, 1030, 23, 1031, 103, 1040, 10, 1041, 102, 1050, 11, 1051,
+    113, 1060, 12, 1061, 111, 1100, 110, 1110, 201, 1120, 200, 1130, 112, 1140, 203, 1150, 20, 1160, 22, 1170, 202, 123, 120, 210,
+    213, 212, 122, 21, 211, 300, 121, 400, 402, 403, 401, 310, 501, 220, 221, 223, 500, 600, 601, 222, 700, 410, 800, 801,
+    413, 411, 412, 802, 803, 511, 320, 804, 805, 806, 900, 901, 610, 510, 902, 903, 611, 904, 420, 905, 422, 150, 906, 421,
+    423, 907, 710, 810, 151, 811, 812, 153, 152, 813, 814, 815, 621, 816, 620, 251, 910, 911, 912, 521, 253, 520, 913, 250,
+    914, 252, 160, 915, 916, 917, 720, 820, 161, 821, 822, 163, 823, 350, 260, 162, 824, 825, 826, 920, 921, 922, 263, 923,
+    924, 925, 170, 926, 171, 927, 172, 261, 173, 262, 453, 451, 270, 452, 450, 551, 550, 271, 272, 273, 360, 370, 460, 461,
+    462, 463, 650, 472, 560, 470, 561, 473, 471, 651, 570, 750, 660, 571, 661, 671, 670, 760, 770,
 )
 
 
-def mlp_kernel(chips, x_hbm, o_hbm, wo_hbm, w1_hbm, w3_hbm, w2_hbm, ga_hbm, gm_hbm, y_out,
-               o_ref, ga_ref, gm_ref, small_sem, wo, w1, w3, w2, x_own, gains, part, pair_in, relay_in, near_in, hid, act, w_sem, x_sem, y_sem, send_sem, recv_sem):
+def mlp_kernel(chips, x_hbm, part_in, w1_hbm, w3_hbm, w2_hbm, ga_hbm, gm_hbm, hid, part,
+               ga_ref, gm_ref, small_sem, w1, w3, w2, x_own, gains, pair_in, relay_in, near_in, act, w_sem, x_sem, send_sem, recv_sem):
     steps, rows, d_model = x_hbm.shape
     ff = w1_hbm.shape[1]
     piece = d_model // QUARTERS
@@ -304,28 +300,25 @@
     right, left, sib = nxt * 2 + core, prv * 2 + core, chip * 2 + 1 - core
     n_gate, n_down = ff // GATE_TILE, d_model // DOWN_TILE
 
-    def cols(hbm, buf, j, width, sem):
-        return pltpu.make_async_copy(hbm.at[:, pl.ds(j * width, width)], buf.at[:, pl.ds(j * width, width)], w_sem.at[sem])
-
-    wo_in = [cols(wo_hbm, wo, j, piece, j) for j in range(QUARTERS)]
-    w1_in = [cols(w1_hbm, w1, j, GATE_TILE, QUARTERS + j) for j in range(n_gate)]
-    w3_in = [cols(w3_hbm, w3, j, GATE_TILE, QUARTERS + n_gate + j) for j in range(n_gate)]
-    w2_in = [cols(w2_hbm, w2, j, DOWN_TILE, QUARTERS + 2 * n_gate + j) for j in range(n_down)]
+    def fetches(hbm, buf, width, sem):
+        depth = hbm.shape[0] // FETCHES
+        return [[pltpu.make_async_copy(hbm.at[pl.ds(i * depth, depth), pl.ds(j * width, width)],
+                                       buf.at[pl.ds(i * depth, depth), pl.ds(j * width, width)], w_sem.at[sem + j * FETCHES + i])
+                 for i in range(FETCHES)] for j in range(hbm.shape[1] // width)]
+
+    w1_in = fetches(w1_hbm, w1, GATE_TILE, 0)
+    w3_in = fetches(w3_hbm, w3, GATE_TILE, n_gate * FETCHES)
+    gate_in = [a + b for a, b in zip(w1_in, w3_in)]
+    down_in = fetches(w2_hbm, w2, DOWN_TILE, 2 * n_gate * FETCHES)
 
     def slot(c, k):
         return pl.ds(pl.multiple_of((c * 2 + k) * SLOT_ROWS, SLOT_ROWS), SLOT_ROWS)
 
     x_in = [pltpu.make_async_copy(x_hbm.at[t, slot(chip, core), :], x_own.at[t], x_sem.at[t]) for t in range(steps)]
     small_in = [pltpu.make_async_copy(src, dst, small_sem.at[i]) for i, (src, dst) in enumerate(
-        ((o_hbm, o_ref), (ga_hbm, ga_ref), (gm_hbm, gm_ref)))]
-    for copy in small_in + wo_in + x_in:
+        ((ga_hbm, ga_ref), (gm_hbm, gm_ref)))]
+    for copy in small_in + x_in:
         copy.start()
-    for j in range(n_gate):
-        w1_in[j].start()
-        w3_in[j].start()
-    for copy in w2_in:
-        copy.start()
-
     barrier = pltpu.get_barrier_semaphore()
     for other in (right, left, sib):
         pl.semaphore_signal(barrier, inc=1, device_id={"tp": other}, device_id_type=MESH)
@@ -385,12 +378,7 @@
         for kind, q in COPIES:
             copy(ph, t, kind, q).wait_send()
 
-    def proj(ph, t, q):
-        if t == 0:
-            wo_in[q].wait()
-        for n in range(q * piece, (q + 1) * piece, DOWN_TILE):
-            val = matmul(o_ref[t], wo[:, n:n + DOWN_TILE]).astype(BF16)
-            part[t, :, :, :, n:n + DOWN_TILE] = val.reshape(chips, 2, SLOT_ROWS, DOWN_TILE)
+    def pair_send(ph, t, q):
         copy(0, t, "pair", q).start()
 
     def pair_add(ph, t, q):
@@ -444,13 +432,11 @@
     def gather(ph, t, _):
         for kind in WHOLE:
             copy(ph, t, kind).wait_recv()
-        if ph == 1:
-            pltpu.make_async_copy(hid.at[t], y_out.at[t], y_sem.at[t]).start()
 
     def gate_up(ph, t, j):
         if t == 0:
-            w1_in[j].wait()
-            w3_in[j].wait()
+            for fetch in gate_in[j]:
+                fetch.wait()
         sl = slice(j * GATE_TILE, (j + 1) * GATE_TILE)
         gate = matmul(hid[t], w1[:, sl])
         up = matmul(hid[t], w3[:, sl])
@@ -460,93 +446,78 @@
         if j == 0:
             sent(0, t)
         if t == 0:
-            w2_in[j].wait()
+            for fetch in down_in[j]:
+                fetch.wait()
         sl = slice(j * DOWN_TILE, (j + 1) * DOWN_TILE)
         val = matmul(act[...], w2[:, sl]).astype(BF16)
         part[t, :, :, :, sl] = val.reshape(chips, 2, SLOT_ROWS, DOWN_TILE)
         if (j + 1) * DOWN_TILE % piece == 0:
             copy(1, t, "pair", (j + 1) * DOWN_TILE // piece - 1).start()
 
-    run = (proj, pair_add, relay_add, norm, pass_on, pass_sib, far_sib, gather, gate_up, down)
+    run = (pair_send, pair_add, relay_add, norm, pass_on, pass_sib, far_sib, gather, gate_up, down)
     for code in ORDER:
-        run[code // 100](code // 50 % 2, code % 50 // 10, code % 10)
+        if code >= 1000:
+            (gate_in, down_in)[code // 100 % 10][code // 10 % 10][code % 10].start()
+        else:
+            run[code // 100](code // 50 % 2, code % 50 // 10, code % 10)
     for t in range(steps):
         sent(1, t)
-        pltpu.make_async_copy(hid.at[t], y_out.at[t], y_sem.at[t]).wait()
-
-
-def run_mlp(tp, x_seq, attn, w_o, w_gate, w_up, w_down, g_attn, g_mlp):
+
+
+def run_mlp(tp, x_seq, part, w_gate, w_up, w_down, g_attn, g_mlp):
     steps, rows, d_model = x_seq.shape
     ff = w_gate.shape[1]
     chips = tp // 2
-    n_sem = QUARTERS + 2 * (ff // GATE_TILE) + d_model // DOWN_TILE
-    return pl.pallas_call(
+    n_sem = (2 * (ff // GATE_TILE) + d_model // DOWN_TILE) * FETCHES
+    hid, _ = pl.pallas_call(
         functools.partial(mlp_kernel, chips),
-        out_shape=jax.ShapeDtypeStruct((steps, rows, d_model), BF16),
-        in_specs=[ANY_SPEC] * 8,
-        out_specs=ANY_SPEC,
+        out_shape=(pltpu.VMEM((steps, rows, d_model), BF16), pltpu.VMEM(part.shape, BF16)),
+        in_specs=[ANY_SPEC, VMEM_SPEC] + [ANY_SPEC] * 5,
+        out_specs=(VMEM_SPEC, VMEM_SPEC),
+        input_output_aliases={1: 1},
         scratch_shapes=[
-            pltpu.VMEM(attn.shape, BF16),
             pltpu.VMEM((d_model // 128, 128), BF16),
             pltpu.VMEM((d_model // 128, 128), BF16),
-            pltpu.SemaphoreType.DMA((3,)),
-            pltpu.VMEM(w_o.shape, BF16),
+            pltpu.SemaphoreType.DMA((2,)),
             pltpu.VMEM(w_gate.shape, BF16),
             pltpu.VMEM(w_up.shape, BF16),
             pltpu.VMEM(w_down.shape, BF16),
             pltpu.VMEM((steps, SLOT_ROWS, d_model), BF16),
             pltpu.VMEM((2, 1, d_model), F32),
-            pltpu.VMEM((steps, chips, 2, SLOT_ROWS, d_model), BF16),
             pltpu.VMEM((steps, chips, SLOT_ROWS, d_model), BF16),
             pltpu.VMEM((steps, SLOT_ROWS, d_model), BF16),
             pltpu.VMEM((steps, 2, SLOT_ROWS, d_model), BF16),
-            pltpu.VMEM((steps, rows, d_model), BF16),
             pltpu.VMEM((rows, ff), BF16),
             pltpu.SemaphoreType.DMA((n_sem,)),
-            pltpu.SemaphoreType.DMA((steps,)),
             pltpu.SemaphoreType.DMA((steps,)),
             pltpu.SemaphoreType.DMA((2, steps, len(COPIES))),
             pltpu.SemaphoreType.DMA((2, steps, len(COPIES))),
         ],
-        compiler_params=pltpu.CompilerParams(collective_id=1, has_side_effects=True, vmem_limit_bytes=VMEM_LIMIT),
+        compiler_params=pltpu.CompilerParams(collective_id=1, has_side_effects=True, vmem_limit_bytes=MLP_VMEM),
         name="mlp",
-    )(x_seq, attn, w_o, w_gate, w_up, w_down, g_attn.reshape(-1, 128), g_mlp.reshape(-1, 128))
-
-
-COPY_ROWS = 64
-
-
-def store_kernel(src, dst, buf, in_sem, out_sem):
-    rows = src.shape[0]
-    n = rows // COPY_ROWS
-    sl = [pl.ds(i * COPY_ROWS, COPY_ROWS) for i in range(n)]
-    ins = [pltpu.make_async_copy(src.at[sl[i]], buf.at[sl[i]], in_sem.at[i]) for i in range(n)]
-    outs = [pltpu.make_async_copy(buf.at[sl[i]], dst.at[sl[i]], out_sem.at[i]) for i in range(n)]
-    for i in range(n):
-        ins[i].start()
-    for i in range(n):
-        ins[i].wait()
-        outs[i].start()
-    for i in range(n):
-        outs[i].wait()
+    )(x_seq, in_vmem(part), w_gate, w_up, w_down, g_attn.reshape(-1, 128), g_mlp.reshape(-1, 128))
+    return hid
+
+
+def store_kernel(src, dst, sem):
+    steps = src.shape[0]
+    copies = [pltpu.make_async_copy(src.at[t], dst.at[t], sem.at[t]) for t in range(steps)]
+    for copy in copies:
+        copy.start()
+    for copy in copies:
+        copy.wait()
 
 
 def run_store(y_seq):
-    steps, rows, d_model = y_seq.shape
-    total = steps * rows
     return pl.pallas_call(
         store_kernel,
-        out_shape=jax.ShapeDtypeStruct((total, d_model), BF16),
-        in_specs=[ANY_SPEC],
+        out_shape=jax.ShapeDtypeStruct(y_seq.shape, BF16),
+        in_specs=[VMEM_SPEC],
         out_specs=ANY_SPEC,
-        scratch_shapes=[
-            pltpu.VMEM((total, d_model), BF16),
-            pltpu.SemaphoreType.DMA((total // COPY_ROWS,)),
-            pltpu.SemaphoreType.DMA((total // COPY_ROWS,)),
-        ],
-        compiler_params=pltpu.CompilerParams(vmem_limit_bytes=VMEM_LIMIT),
+        scratch_shapes=[pltpu.SemaphoreType.DMA((y_seq.shape[0],))],
+        compiler_params=pltpu.CompilerParams(vmem_limit_bytes=16 * 1024 * 1024),
         name="store",
-    )(y_seq.reshape(total, d_model)).reshape(y_seq.shape)
+    )(in_vmem(y_seq))
 
 
 def solution(mesh):
@@ -554,10 +525,11 @@
 
     def local_run(x_seq, cache_len, k_cache, v_cache, w_q, w_k, w_v, w_o, w_gate, w_up, w_down, g_q, g_k, g_attn, g_mlp):
         heads = w_q.shape[1] // w_k.shape[1]
-        q_rows, k_new, v_new = run_qkv(tp, x_seq, cache_len, w_q, w_k, w_v, g_q, g_k)
-        attn, k_out, v_out = run_attention(heads, cache_len, q_rows, k_new, v_new, k_cache, v_cache)
-        y_seq = run_mlp(tp, x_seq, attn, w_o, w_gate, w_up, w_down, g_attn, g_mlp)
-        return run_store(y_seq), k_out, v_out
+        flat = (k_cache.shape[0],) + k_cache.shape[2:]
+        q_rows, k_new, v_new, k_old, v_old = run_qkv(tp, x_seq, cache_len, w_q, w_k, w_v, g_q, g_k, k_cache.reshape(flat), v_cache.reshape(flat))
+        part, k_out, v_out = run_attention(tp, heads, cache_len, q_rows, k_new, v_new, k_old, v_old, w_o)
+        y_seq = run_mlp(tp, x_seq, part, w_gate, w_up, w_down, g_attn, g_mlp)
+        return run_store(y_seq), k_out.reshape(k_cache.shape), v_out.reshape(v_cache.shape)
 
     data_spec = P(None, 'dp', None)
     cache_spec = P('dp', 'tp', None, None)

time: 119 us -> 109 us (0.916)
  Pallas kernels: 118 us -> 101 us
  local copies, waits for them, and re-layouts: 0 us -> 6.78 us
    pallas_call x2, Pallas kernels: 87.4 us -> 72.3 us  [the longest x1 70.6 us: run_mlp(): pl.pallas_call(functools.partial(mlp_kernel, chips), out_shape=(pltpu.VME...]
    unnamed x0 -> x8, local copies, waits for them, and re-layouts: none -> 6.78 us
    pallas_call x1, Pallas kernels: 13.5 us -> 12 us  [run_attention(): pl.pallas_call(functools.partial(attention_kernel, steps, heads), out_sha...]
where the time goes in v5:
time: 109 us
  Pallas kernels  101 us (93%)
  local copies, waits for them, and re-layouts  6.78 us (6%)
    pallas_call x1, Pallas kernels, run_mlp(): pl.pallas_call(functools.partial(mlp_kernel, chips), out_shape=(pltpu.VME...  70.6 us
    pallas_call x1, Pallas kernels, run_qkv(): pl.pallas_call(functools.partial(qkv_kernel, tp, width * tp, hd * tp), ou...  17 us
    pallas_call x1, Pallas kernels, run_attention(): pl.pallas_call(functools.partial(attention_kernel, steps, heads), out_sha...  12 us
    unnamed x8, local copies, waits for them, and re-layouts  6.78 us

profile of v5, /device:TPU:81, one launch (start us, length us, event | category | flops | bytes accessed | tf_op | source)
XLA Modules:
  0.0 108.9 jit_solution(5275900968382277452)
XLA Ops:
  0.6 0.0 copy-start.2
  0.6 0.0 copy-start.3
  0.7 17.0 %qkv.1 = (bf16[128,16,128]{2,1,0:T(8,128)(2,1)S(1)}, f32[3,128,128]{2,1,0:T(8,128)S(1)}, f32[3,128,128]{2,1,0:T(8,128)S(1)}, bf16[128,256,128]{2,1,0:T(8,128)(2,1)S(1)}, bf16[128,256,128]{2,1,0:T(8,128)(2,1)S(1)}) custom-call(bf16[3,128,4096]{2,1,0:T(8,128)(2,1)} %x_hbm.3, s32[1,128]{1,0:T(1,128)} %bitcast.13, f32[1,128]{1,0:T(1,128)} %constant.2.clone.freq_hbm, ...), custom_call_target="tpu_custom_call" | custom-call | tf_op jit(solution)/shard_map/qkv/pallas_call | solution.py:139
  17.7 0.0 copy-start
  17.7 3.4 %copy-done = bf16[128,256,128]{2,1,0:T(8,128)(2,1)} copy-done((bf16[128,256,128]{2,1,0:T(8,128)(2,1)}, bf16[128,256,128]{2,1,0:T(8,128)(2,1)S(1)}, u32[]{:S(2)}) %copy-start) | copy-done | bytes 8388632
  21.1 0.0 copy-done.2
  21.1 0.0 copy-done.3
  21.1 0.0 copy-start.1
  21.1 3.4 %copy-done.1 = bf16[128,256,128]{2,1,0:T(8,128)(2,1)S(1)} copy-done((bf16[128,256,128]{2,1,0:T(8,128)(2,1)S(1)}, bf16[128,256,128]{2,1,0:T(8,128)(2,1)}, u32[]{:S(2)}) %copy-start.1) | copy-done | bytes 8388632
  24.5 12.0 %attention.1 = (bf16[128,256,128]{2,1,0:T(8,128)(2,1)}, bf16[128,256,128]{2,1,0:T(8,128)(2,1)}, bf16[128,256,128]{2,1,0:T(8,128)(2,1)S(1)}, bf16[128,256,128]{2,...) custom-call(s32[128]{0:T(128)S(1)} %copy-done.3, ...), custom_call_target="tpu_custom_call", output_to_operand_aliasing={{2}: (4, {}), {3}: (5, {})} | custom-call | tf_op jit(solution)/shard_map/attention/pallas_call | solution.py:251
  36.5 70.6 %mlp.1 = (bf16[3,128,4096]{2,1,0:T(8,128)(2,1)S(1)}, bf16[3,4,2,16,4096]{4,3,2,1,0:T(8,128)(2,1)S(1)}) custom-call(bf16[3,128,4096]{2,1,0:T(8,128)(2,1)} %x_hbm.3, bf16[3,4,2,16,4096]{4,3,2,1,0:T(8,128)(2,1)S(1)} %get-tuple-element.17.part_in, bf16[4096,1792]{1,0:T(8,128)(2,1)} %w1_hbm.1, ...), custom_call_target="tpu_custom_call", output_to_operand_aliasing={{1}: (1, {})} | custom-call | tf_op jit(solution)/shard_map/mlp/pallas_call | solution.py:472
  107.1 1.7 %store.1 = bf16[3,128,4096]{2,1,0:T(8,128)(2,1)} custom-call(bf16[3,128,4096]{2,1,0:T(8,128)(2,1)S(1)} %get-tuple-element.18.src), custom_call_target="tpu_custom_call" | custom-call | tf_op jit(solution)/shard_map/store/pallas_call | solution.py:512
Async XLA Ops:
  0.6 20.4 %copy-start.2 = (bf16[512,4096]{1,0:T(8,128)(2,1)S(1)}, bf16[512,4096]{1,0:T(8,128)(2,1)}, u32[]{:S(2)}) copy-start(bf16[512,4096]{1,0:T(8,128)(2,1)} %wo_hbm.1) | copy-start | bytes 12582916
  0.6 20.4 %copy-start.3 = (s32[128]{0:T(128)S(1)}, s32[128]{0:T(128)}, u32[]{:S(2)}) copy-start(s32[128]{0:T(128)} %len_ref.1) | copy-start | bytes 1540
  17.7 3.4 %copy-start = (bf16[128,256,128]{2,1,0:T(8,128)(2,1)}, bf16[128,256,128]{2,1,0:T(8,128)(2,1)S(1)}, u32[]{:S(2)}) copy-start(bf16[128,256,128]{2,1,0:T(8,128)(2,1)S(1)} %get-tuple-element.15.k_in) | copy-start | bytes 25165828
  21.1 3.4 %copy-start.1 = (bf16[128,256,128]{2,1,0:T(8,128)(2,1)S(1)}, bf16[128,256,128]{2,1,0:T(8,128)(2,1)}, u32[]{:S(2)}) copy-start(bf16[128,256,128]{2,1,0:T(8,128)(2,1)} %copy-done) | copy-start | bytes 25165828

commit v6 on v5

--- a/solution.py
+++ b/solution.py
@@ -16,9 +16,9 @@
 VMEM_SPEC = pl.BlockSpec(memory_space=pltpu.VMEM)
 ANY_SPEC = pl.BlockSpec(memory_space=pl.ANY)
 SMEM_SPEC = pl.BlockSpec(memory_space=pltpu.SMEM)
-QKV_VMEM = 40 * 1024 * 1024
+QKV_VMEM = 16 * 1024 * 1024
 ATTENTION_VMEM = 24 * 1024 * 1024
-MLP_VMEM = 54 * 1024 * 1024
+MLP_VMEM = 50 * 1024 * 1024
 SLOT_ROWS = 16
 
 
@@ -26,6 +26,10 @@
     return pltpu.with_memory_space_constraint(val, pltpu.VMEM)
 
 
+def in_hbm(val):
+    return pltpu.with_memory_space_constraint(val, pltpu.HBM)
+
+
 def matmul(lhs, rhs):
     return jnp.dot(lhs, rhs, preferred_element_type=F32)
 
@@ -35,25 +39,23 @@
 
 def qkv_kernel(tp, q_width, kv_width, x_hbm, len_hbm, freq_hbm, wq_hbm, wk_hbm, wv_hbm, gq_hbm, gk_hbm, kc_hbm, vc_hbm,
                q_out, kn_out, vn_out, kc_out, vc_out,
-               len_ref, freq_ref, gq_ref, gk_ref, small_sem, cache_sem, x_buf, wq_buf, wk_buf, wv_buf, q_raw, q_rows, part, inbox, turn, in_sem, send_sem, recv_sem):
+               len_ref, freq_ref, gq_ref, gk_ref, small_sem, cache_sem, x_buf, wq_buf, wkv_buf, q_raw, k_raw, q_rows, part, inbox, turn, in_sem, send_sem, recv_sem):
     steps, rows, _ = x_hbm.shape
     hd = wk_hbm.shape[1]
     heads = wq_hbm.shape[1] // hd
     pad = q_out.shape[1]
     me = lax.axis_index("tp")
     x_in = [pltpu.make_async_copy(x_hbm.at[t], x_buf.at[pl.ds(t * rows, rows), :], in_sem.at[t]) for t in range(steps)]
-    for copy in x_in:
-        copy.start()
     half = heads * hd // 2
-    wk_in = pltpu.make_async_copy(wk_hbm, wk_buf, in_sem.at[3])
+    wk_in = pltpu.make_async_copy(wk_hbm, wkv_buf.at[:, pl.ds(0, hd)], in_sem.at[3])
     wq_in = [pltpu.make_async_copy(wq_hbm.at[:, pl.ds(j * half, half)], wq_buf.at[:, pl.ds(j * half, half)], in_sem.at[4 + j]) for j in range(2)]
-    wv_in = pltpu.make_async_copy(wv_hbm, wv_buf, in_sem.at[6])
+    wv_in = pltpu.make_async_copy(wv_hbm, wkv_buf.at[:, pl.ds(hd, hd)], in_sem.at[6])
     small_in = [pltpu.make_async_copy(src, dst, small_sem.at[i]) for i, (src, dst) in enumerate(
         ((len_hbm, len_ref), (freq_hbm, freq_ref), (gq_hbm, gq_ref), (gk_hbm, gk_ref)))]
     seqs = rows // CACHE_PARTS
     cache_in = [pltpu.make_async_copy(src.at[pl.ds(i * seqs, seqs)], dst.at[pl.ds(i * seqs, seqs)], cache_sem.at[c, i])
                 for i in range(CACHE_PARTS) for c, (src, dst) in enumerate(((kc_hbm, kc_out), (vc_hbm, vc_out)))]
-    for copy in small_in + [wk_in, wq_in[0], wq_in[1], wv_in]:
+    for copy in [wk_in, wv_in] + x_in + small_in + wq_in:
         copy.start()
 
     barrier = pltpu.get_barrier_semaphore()
@@ -71,11 +73,15 @@
         tables.append((jnp.cos(angle), jnp.sin(angle) * sign))
 
     q_rows[...] = jnp.zeros_like(q_rows)
-    for copy in x_in:
-        copy.wait()
     wk_in.wait()
-    k_raw = matmul(x_buf[...], wk_buf[...]).astype(BF16).astype(F32)
-    k_sq = jnp.sum(k_raw * k_raw, axis=1, keepdims=True)
+    wv_in.wait()
+    k_sq = []
+    for t in range(steps):
+        x_in[t].wait()
+        val = matmul(x_buf[t * rows:(t + 1) * rows, :], wkv_buf[...]).astype(BF16).astype(F32)
+        k_raw[t] = val[:, :hd]
+        vn_out[t] = val[:, hd:]
+        k_sq.append(jnp.sum(val[:, :hd] * val[:, :hd], axis=1, keepdims=True))
     q_sq = None
     for j in range(2):
         wq_in[j].wait()
@@ -89,7 +95,7 @@
     col = lax.broadcasted_iota(jnp.int32, (rows, rows), 1)
     for t in range(steps):
         packed = jnp.where(col == t, q_sq[t * rows:(t + 1) * rows], packed)
-        packed = jnp.where(col == steps + t, k_sq[t * rows:(t + 1) * rows], packed)
+        packed = jnp.where(col == steps + t, k_sq[t], packed)
     part[...] = jnp.transpose(packed)[:part.shape[0]]
     pl.semaphore_wait(barrier, tp - 1)
     copies = []
@@ -101,8 +107,6 @@
         copies.append(copy)
     for copy in cache_in[1:]:
         copy.start()
-    wv_in.wait()
-    vn_out[...] = matmul(x_buf[...], wv_buf[...]).astype(BF16).astype(F32).reshape(steps, rows, hd)
     total = part[...]
     for j in range(1, tp):
         copies[j - 1].wait()
@@ -116,7 +120,7 @@
         cos_tab, sin_tab = tables[t]
         q_fac = lax.rsqrt(sums[:, t:t + 1] / q_width + NORM_EPS)
         k_fac = lax.rsqrt(sums[:, steps + t:steps + t + 1] / kv_width + NORM_EPS)
-        val = k_raw[t * rows:(t + 1) * rows] * k_fac * gain_k
+        val = k_raw[t] * k_fac * gain_k
         val = val * cos_tab + pltpu.roll(val, hd // 2, axis=1) * sin_tab
         kn_out[t] = val.astype(BF16).astype(F32)
         for g in range(heads):
@@ -154,9 +158,9 @@
             pltpu.SemaphoreType.DMA((2, CACHE_PARTS)),
             pltpu.VMEM((steps * rows, d_model), BF16),
             pltpu.VMEM((d_model, width), BF16),
-            pltpu.VMEM((d_model, hd), BF16),
-            pltpu.VMEM((d_model, hd), BF16),
+            pltpu.VMEM((d_model, 2 * hd), BF16),
             pltpu.VMEM((steps * rows, width), F32),
+            pltpu.VMEM((steps, rows, hd), F32),
             pltpu.VMEM((rows * pad, hd), F32),
             pltpu.VMEM((8, rows), F32),
             pltpu.VMEM((tp - 1, 8, rows), F32),
@@ -167,15 +171,15 @@
         ],
         compiler_params=pltpu.CompilerParams(collective_id=0, has_side_effects=True, vmem_limit_bytes=QKV_VMEM),
         name="qkv",
-    )(x_seq, cache_len.reshape(1, rows), freq, w_q, w_k, w_v, g_q.reshape(heads, hd), g_k.reshape(1, hd), k_cache, v_cache)
+    )(*[in_hbm(val) for val in (x_seq, cache_len.reshape(1, rows), freq, w_q, w_k, w_v, g_q.reshape(heads, hd), g_k.reshape(1, hd), k_cache, v_cache)])
 
 
 SEQ_BLOCK = 8
 PATCH_ROWS = 32
 
 
-def attention_kernel(steps, heads, len_ref, q_ref, kn_ref, vn_ref, k_in, v_in, wo_hbm, k_out, v_out, k_buf, v_buf, part,
-                     o_ref, wo, mixed, wo_sem, out_sem):
+def attention_kernel(steps, heads, len_ref, q_ref, kn_ref, vn_ref, k_in, v_in, wo_hbm, k_out, v_out, part,
+                     k_buf, v_buf, o_ref, wo, mixed, wo_sem, out_sem):
     rows, seq_max, hd = k_buf.shape
     pad = q_ref.shape[1]
     blocks = rows // SEQ_BLOCK
@@ -195,6 +199,9 @@
     key_off = key_col - step_row
 
     def body(blk, carry):
+        block = pl.ds(blk * SEQ_BLOCK, SEQ_BLOCK)
+        k_buf[block] = k_in[block]
+        v_buf[block] = v_in[block]
         lens = []
         for i in range(SEQ_BLOCK):
             b = blk * SEQ_BLOCK + i
@@ -246,15 +253,15 @@
     steps = k_new.shape[0]
     pad = q_rows.shape[1]
     flat = jax.ShapeDtypeStruct(k_cache.shape, BF16)
-    held = pltpu.VMEM(k_cache.shape, BF16)
     part = pltpu.VMEM((steps, tp // 2, 2, rows // tp, w_o.shape[1]), BF16)
-    k_out, v_out, _, _, part = pl.pallas_call(
+    k_out, v_out, part = pl.pallas_call(
         functools.partial(attention_kernel, steps, heads),
-        out_shape=(flat, flat, held, held, part),
+        out_shape=(flat, flat, part),
         in_specs=[SMEM_SPEC] + [VMEM_SPEC] * 5 + [ANY_SPEC],
-        out_specs=(ANY_SPEC, ANY_SPEC, VMEM_SPEC, VMEM_SPEC, VMEM_SPEC),
-        input_output_aliases={4: 2, 5: 3},
+        out_specs=(ANY_SPEC, ANY_SPEC, VMEM_SPEC),
         scratch_shapes=[
+            pltpu.VMEM(k_cache.shape, BF16),
+            pltpu.VMEM(v_cache.shape, BF16),
             pltpu.VMEM((steps * rows, heads * hd), BF16),
             pltpu.VMEM(w_o.shape, BF16),
             pltpu.VMEM((rows * pad, hd), F32),
@@ -263,7 +270,7 @@
         ],
         compiler_params=pltpu.CompilerParams(vmem_limit_bytes=ATTENTION_VMEM),
         name="attention",
-    )(cache_len, in_vmem(q_rows), in_vmem(k_new), in_vmem(v_new), in_vmem(k_cache), in_vmem(v_cache), w_o)
+    )(cache_len, in_vmem(q_rows), in_vmem(k_new), in_vmem(v_new), in_vmem(k_cache), in_vmem(v_cache), in_hbm(w_o))
     return part, k_out, v_out
 
 
@@ -278,14 +285,14 @@
 DOWN_TILE = 512
 TASKS = ("send", "pair", "relay", "norm", "pass", "sib", "sibf", "gather", "gate", "down", "fetch")
 ORDER = (
-    0, 1000, 1, 1001, 3, 1010, 100, 1011, 2, 1020, 101, 1021, 13, 1030, 23, 1031, 103, 1040, 10, 1041, 102, 1050, 11, 1051,
-    113, 1060, 12, 1061, 111, 1100, 110, 1110, 201, 1120, 200, 1130, 112, 1140, 203, 1150, 20, 1160, 22, 1170, 202, 123, 120, 210,
-    213, 212, 122, 21, 211, 300, 121, 400, 402, 403, 401, 310, 501, 220, 221, 223, 500, 600, 601, 222, 700, 410, 800, 801,
-    413, 411, 412, 802, 803, 511, 320, 804, 805, 806, 900, 901, 610, 510, 902, 903, 611, 904, 420, 905, 422, 150, 906, 421,
-    423, 907, 710, 810, 151, 811, 812, 153, 152, 813, 814, 815, 621, 816, 620, 251, 910, 911, 912, 521, 253, 520, 913, 250,
-    914, 252, 160, 915, 916, 917, 720, 820, 161, 821, 822, 163, 823, 350, 260, 162, 824, 825, 826, 920, 921, 922, 263, 923,
-    924, 925, 170, 926, 171, 927, 172, 261, 173, 262, 453, 451, 270, 452, 450, 551, 550, 271, 272, 273, 360, 370, 460, 461,
-    462, 463, 650, 472, 560, 470, 561, 473, 471, 651, 570, 750, 660, 571, 661, 671, 670, 760, 770,
+    2, 21, 1, 3, 1060, 23, 11, 0, 102, 13, 1150, 103, 1160, 12, 100, 101, 1051, 10, 1041, 112, 110, 1110, 113, 202,
+    1011, 20, 111, 200, 1100, 203, 201, 123, 212, 22, 121, 120, 211, 1021, 210, 1140, 213, 300, 122, 1130, 1000, 1030, 400, 402,
+    401, 403, 1040, 310, 221, 220, 1050, 1170, 223, 1120, 1020, 222, 501, 500, 1001, 600, 601, 1010, 412, 410, 1061, 1031, 700, 800,
+    801, 802, 411, 413, 803, 804, 320, 805, 511, 806, 900, 901, 510, 902, 610, 611, 903, 904, 150, 905, 906, 710, 422, 151,
+    907, 810, 420, 421, 811, 153, 812, 152, 520, 423, 813, 814, 251, 250, 521, 815, 816, 910, 911, 620, 912, 913, 253, 252,
+    914, 160, 621, 915, 916, 161, 917, 720, 820, 821, 162, 822, 163, 823, 350, 824, 825, 826, 920, 921, 262, 922, 923, 261,
+    924, 170, 925, 926, 171, 927, 260, 172, 173, 263, 452, 451, 270, 453, 450, 272, 271, 273, 360, 370, 460, 551, 650, 463,
+    462, 651, 461, 550, 470, 472, 473, 750, 471, 570, 661, 660, 571, 560, 561, 670, 671, 760, 770,
 )
 
 
@@ -495,7 +502,7 @@
         ],
         compiler_params=pltpu.CompilerParams(collective_id=1, has_side_effects=True, vmem_limit_bytes=MLP_VMEM),
         name="mlp",
-    )(x_seq, in_vmem(part), w_gate, w_up, w_down, g_attn.reshape(-1, 128), g_mlp.reshape(-1, 128))
+    )(in_hbm(x_seq), in_vmem(part), in_hbm(w_gate), in_hbm(w_up), in_hbm(w_down), g_attn.reshape(-1, 128), g_mlp.reshape(-1, 128))
     return hid
 
 

time: 109 us -> 103 us (0.945)
  local copies, waits for them, and re-layouts: 6.78 us -> 0.01 us
    unnamed x8 -> x2, local copies, waits for them, and re-layouts: 6.78 us -> 0.01 us
where the time goes in v6:
time: 103 us
  Pallas kernels  102 us (99%)
    pallas_call x1, Pallas kernels, run_mlp(): pl.pallas_call(functools.partial(mlp_kernel, chips), out_shape=(pltpu.VME...  70.9 us
    pallas_call x1, Pallas kernels, run_qkv(): pl.pallas_call(functools.partial(qkv_kernel, tp, width * tp, hd * tp), ou...  16.9 us
    pallas_call x1, Pallas kernels, run_attention(): pl.pallas_call(functools.partial(attention_kernel, steps, heads), out_sha...  12.6 us

profile of v6, /device:TPU:81, one launch (start us, length us, event | category | flops | bytes accessed | tf_op | source)
XLA Modules:
  0.0 102.9 jit_solution(334326391594981200)
XLA Ops:
  0.6 0.0 copy-start
  0.6 16.9 %qkv.1 = (bf16[128,16,128]{2,1,0:T(8,128)(2,1)S(1)}, f32[3,128,128]{2,1,0:T(8,128)S(1)}, f32[3,128,128]{2,1,0:T(8,128)S(1)}, bf16[128,256,128]{2,1,0:T(8,128)(2,1)S(1)}, bf16[128,256,128]{2,1,0:T(8,128)(2,1)S(1)}) custom-call(bf16[3,128,4096]{2,1,0:T(8,128)(2,1)} %x_hbm.3, s32[1,128]{1,0:T(1,128)} %bitcast.13, f32[1,128]{1,0:T(1,128)} %constant.2.clone.freq_hbm, ...), custom_call_target="tpu_custom_call" | custom-call | tf_op jit(solution)/shard_map/qkv/pallas_call | solution.py:143
  17.5 0.0 copy-done
  17.5 12.6 %attention.1 = (bf16[128,256,128]{2,1,0:T(8,128)(2,1)}, bf16[128,256,128]{2,1,0:T(8,128)(2,1)}, bf16[3,4,2,16,4096]{4,3,2,1,0:T(8,128)(2,1)S(1)}) custom-call(s32[128]{0:T(128)S(1)} %copy-done, bf16[128,16,128]{2,1,0:T(8,128)(2,1)S(1)} %get-tuple-element.12.q_ref, f32[3,128,128]{2,1,0:T(8,128)S(1)} %get-tuple-element.13.kn_ref, ...), custom_call_target="tpu_custom_call" | custom-call | tf_op jit(solution)/shard_map/attention/pallas_call | solution.py:257
  30.2 70.9 %mlp.1 = (bf16[3,128,4096]{2,1,0:T(8,128)(2,1)S(1)}, bf16[3,4,2,16,4096]{4,3,2,1,0:T(8,128)(2,1)S(1)}) custom-call(bf16[3,128,4096]{2,1,0:T(8,128)(2,1)} %x_hbm.3, bf16[3,4,2,16,4096]{4,3,2,1,0:T(8,128)(2,1)S(1)} %get-tuple-element.17.part_in, bf16[4096,1792]{1,0:T(8,128)(2,1)} %w1_hbm.1, ...), custom_call_target="tpu_custom_call", output_to_operand_aliasing={{1}: (1, {})} | custom-call | tf_op jit(solution)/shard_map/mlp/pallas_call | solution.py:479
  101.0 1.7 %store.1 = bf16[3,128,4096]{2,1,0:T(8,128)(2,1)} custom-call(bf16[3,128,4096]{2,1,0:T(8,128)(2,1)S(1)} %get-tuple-element.18.src), custom_call_target="tpu_custom_call" | custom-call | tf_op jit(solution)/shard_map/store/pallas_call | solution.py:519
Async XLA Ops:
  0.6 16.9 %copy-start = (s32[128]{0:T(128)S(1)}, s32[128]{0:T(128)}, u32[]{:S(2)}) copy-start(s32[128]{0:T(128)} %len_ref.1) | copy-start | bytes 1540

commit v7 on v6

--- a/solution.py
+++ b/solution.py
@@ -39,7 +39,7 @@
 
 def qkv_kernel(tp, q_width, kv_width, x_hbm, len_hbm, freq_hbm, wq_hbm, wk_hbm, wv_hbm, gq_hbm, gk_hbm, kc_hbm, vc_hbm,
                q_out, kn_out, vn_out, kc_out, vc_out,
-               len_ref, freq_ref, gq_ref, gk_ref, small_sem, cache_sem, x_buf, wq_buf, wkv_buf, q_raw, k_raw, q_rows, part, inbox, turn, in_sem, send_sem, recv_sem):
+               len_ref, freq_ref, gq_ref, gk_ref, small_sem, cache_sem, x_buf, wq_buf, wk_buf, wv_buf, q_raw, k_raw, q_rows, part, inbox, turn, in_sem, send_sem, recv_sem):
     steps, rows, _ = x_hbm.shape
     hd = wk_hbm.shape[1]
     heads = wq_hbm.shape[1] // hd
@@ -47,15 +47,15 @@
     me = lax.axis_index("tp")
     x_in = [pltpu.make_async_copy(x_hbm.at[t], x_buf.at[pl.ds(t * rows, rows), :], in_sem.at[t]) for t in range(steps)]
     half = heads * hd // 2
-    wk_in = pltpu.make_async_copy(wk_hbm, wkv_buf.at[:, pl.ds(0, hd)], in_sem.at[3])
-    wq_in = [pltpu.make_async_copy(wq_hbm.at[:, pl.ds(j * half, half)], wq_buf.at[:, pl.ds(j * half, half)], in_sem.at[4 + j]) for j in range(2)]
-    wv_in = pltpu.make_async_copy(wv_hbm, wkv_buf.at[:, pl.ds(hd, hd)], in_sem.at[6])
+    wk_in = pltpu.make_async_copy(wk_hbm, wk_buf, in_sem.at[3])
+    wq_in = pltpu.make_async_copy(wq_hbm, wq_buf, in_sem.at[5])
+    wv_in = pltpu.make_async_copy(wv_hbm, wv_buf, in_sem.at[4])
     small_in = [pltpu.make_async_copy(src, dst, small_sem.at[i]) for i, (src, dst) in enumerate(
         ((len_hbm, len_ref), (freq_hbm, freq_ref), (gq_hbm, gq_ref), (gk_hbm, gk_ref)))]
     seqs = rows // CACHE_PARTS
     cache_in = [pltpu.make_async_copy(src.at[pl.ds(i * seqs, seqs)], dst.at[pl.ds(i * seqs, seqs)], cache_sem.at[c, i])
                 for i in range(CACHE_PARTS) for c, (src, dst) in enumerate(((kc_hbm, kc_out), (vc_hbm, vc_out)))]
-    for copy in [wk_in, wv_in] + x_in + small_in + wq_in:
+    for copy in [wk_in, wv_in] + x_in + small_in + [wq_in]:
         copy.start()
 
     barrier = pltpu.get_barrier_semaphore()
@@ -75,17 +75,18 @@
     q_rows[...] = jnp.zeros_like(q_rows)
     wk_in.wait()
     wv_in.wait()
+    w_kv = jnp.concatenate([wk_buf[...], wv_buf[...]], axis=1)
     k_sq = []
     for t in range(steps):
         x_in[t].wait()
-        val = matmul(x_buf[t * rows:(t + 1) * rows, :], wkv_buf[...]).astype(BF16).astype(F32)
+        val = matmul(x_buf[t * rows:(t + 1) * rows, :], w_kv).astype(BF16).astype(F32)
         k_raw[t] = val[:, :hd]
         vn_out[t] = val[:, hd:]
         k_sq.append(jnp.sum(val[:, :hd] * val[:, :hd], axis=1, keepdims=True))
     q_sq = None
     for j in range(2):
-        wq_in[j].wait()
-        if j == 1:
+        if j == 0:
+            wq_in.wait()
             cache_in[0].start()
         val = matmul(x_buf[...], wq_buf[:, j * half:(j + 1) * half]).astype(BF16).astype(F32)
         q_raw[:, j * half:(j + 1) * half] = val
@@ -158,7 +159,8 @@
             pltpu.SemaphoreType.DMA((2, CACHE_PARTS)),
             pltpu.VMEM((steps * rows, d_model), BF16),
             pltpu.VMEM((d_model, width), BF16),
-            pltpu.VMEM((d_model, 2 * hd), BF16),
+            pltpu.VMEM((d_model, hd), BF16),
+            pltpu.VMEM((d_model, hd), BF16),
             pltpu.VMEM((steps * rows, width), F32),
             pltpu.VMEM((steps, rows, hd), F32),
             pltpu.VMEM((rows * pad, hd), F32),
@@ -281,18 +283,18 @@
 WHOLE = ("own_s", "sib_r", "sib_l", "sib_fr", "sib_fl")
 COPIES = tuple((kind, q) for kind in PIECED for q in range(QUARTERS)) + tuple((kind, 0) for kind in WHOLE)
 GATE_TILE = 256
-FETCHES = 1
+FETCHES = 8
 DOWN_TILE = 512
 TASKS = ("send", "pair", "relay", "norm", "pass", "sib", "sibf", "gather", "gate", "down", "fetch")
 ORDER = (
-    2, 21, 1, 3, 1060, 23, 11, 0, 102, 13, 1150, 103, 1160, 12, 100, 101, 1051, 10, 1041, 112, 110, 1110, 113, 202,
-    1011, 20, 111, 200, 1100, 203, 201, 123, 212, 22, 121, 120, 211, 1021, 210, 1140, 213, 300, 122, 1130, 1000, 1030, 400, 402,
-    401, 403, 1040, 310, 221, 220, 1050, 1170, 223, 1120, 1020, 222, 501, 500, 1001, 600, 601, 1010, 412, 410, 1061, 1031, 700, 800,
-    801, 802, 411, 413, 803, 804, 320, 805, 511, 806, 900, 901, 510, 902, 610, 611, 903, 904, 150, 905, 906, 710, 422, 151,
-    907, 810, 420, 421, 811, 153, 812, 152, 520, 423, 813, 814, 251, 250, 521, 815, 816, 910, 911, 620, 912, 913, 253, 252,
-    914, 160, 621, 915, 916, 161, 917, 720, 820, 821, 162, 822, 163, 823, 350, 824, 825, 826, 920, 921, 262, 922, 923, 261,
-    924, 170, 925, 926, 171, 927, 260, 172, 173, 263, 452, 451, 270, 453, 450, 272, 271, 273, 360, 370, 460, 551, 650, 463,
-    462, 651, 461, 550, 470, 472, 473, 750, 471, 570, 661, 660, 571, 560, 561, 670, 671, 760, 770,
+    1105, 2, 3, 1, 22, 0, 1101, 102, 101, 11, 10, 1011, 13, 103, 100, 122, 1107, 111, 1007, 1003, 1106, 1004, 12, 113,
+    21, 1012, 201, 202, 1006, 203, 200, 110, 23, 1015, 112, 20, 1008, 120, 211, 123, 1100, 213, 1010, 300, 1102, 1000, 121, 210,
+    1104, 1005, 212, 1009, 402, 400, 1013, 403, 401, 1103, 220, 222, 1002, 500, 501, 1014, 221, 223, 310, 1001, 601, 600, 700, 800,
+    801, 802, 410, 412, 413, 411, 803, 320, 804, 805, 510, 806, 900, 511, 901, 902, 903, 904, 610, 611, 905, 150, 906, 907,
+    422, 423, 710, 151, 420, 421, 810, 152, 153, 811, 812, 520, 813, 814, 815, 251, 816, 250, 910, 911, 912, 521, 913, 253,
+    621, 620, 914, 252, 160, 915, 916, 917, 720, 161, 820, 821, 162, 163, 822, 823, 350, 824, 825, 826, 920, 921, 922, 263,
+    923, 260, 924, 170, 925, 926, 171, 927, 450, 172, 261, 173, 262, 452, 451, 270, 453, 271, 272, 273, 360, 370, 463, 650,
+    651, 550, 460, 461, 462, 470, 472, 471, 561, 551, 473, 570, 750, 560, 571, 660, 661, 760, 670, 671, 770,
 )
 
 
@@ -307,16 +309,13 @@
     right, left, sib = nxt * 2 + core, prv * 2 + core, chip * 2 + 1 - core
     n_gate, n_down = ff // GATE_TILE, d_model // DOWN_TILE
 
-    def fetches(hbm, buf, width, sem):
+    def fetches(hbm, buf, sem):
         depth = hbm.shape[0] // FETCHES
-        return [[pltpu.make_async_copy(hbm.at[pl.ds(i * depth, depth), pl.ds(j * width, width)],
-                                       buf.at[pl.ds(i * depth, depth), pl.ds(j * width, width)], w_sem.at[sem + j * FETCHES + i])
-                 for i in range(FETCHES)] for j in range(hbm.shape[1] // width)]
-
-    w1_in = fetches(w1_hbm, w1, GATE_TILE, 0)
-    w3_in = fetches(w3_hbm, w3, GATE_TILE, n_gate * FETCHES)
-    gate_in = [a + b for a, b in zip(w1_in, w3_in)]
-    down_in = fetches(w2_hbm, w2, DOWN_TILE, 2 * n_gate * FETCHES)
+        blocks = [pl.ds(i * depth, depth) for i in range(FETCHES)]
+        return [pltpu.make_async_copy(hbm.at[blocks[i]], buf.at[blocks[i]], w_sem.at[sem, i]) for i in range(FETCHES)]
+
+    gate_in = [copy for pair in zip(fetches(w1_hbm, w1, 0), fetches(w3_hbm, w3, 1)) for copy in pair]
+    down_in = fetches(w2_hbm, w2, 2)
 
     def slot(c, k):
         return pl.ds(pl.multiple_of((c * 2 + k) * SLOT_ROWS, SLOT_ROWS), SLOT_ROWS)
@@ -441,8 +440,8 @@
             copy(ph, t, kind).wait_recv()
 
     def gate_up(ph, t, j):
-        if t == 0:
-            for fetch in gate_in[j]:
+        if t == 0 and j == 0:
+            for fetch in gate_in:
                 fetch.wait()
         sl = slice(j * GATE_TILE, (j + 1) * GATE_TILE)
         gate = matmul(hid[t], w1[:, sl])
@@ -452,8 +451,8 @@
     def down(ph, t, j):
         if j == 0:
             sent(0, t)
-        if t == 0:
-            for fetch in down_in[j]:
+        if t == 0 and j == 0:
+            for fetch in down_in:
                 fetch.wait()
         sl = slice(j * DOWN_TILE, (j + 1) * DOWN_TILE)
         val = matmul(act[...], w2[:, sl]).astype(BF16)
@@ -464,7 +463,7 @@
     run = (pair_send, pair_add, relay_add, norm, pass_on, pass_sib, far_sib, gather, gate_up, down)
     for code in ORDER:
         if code >= 1000:
-            (gate_in, down_in)[code // 100 % 10][code // 10 % 10][code % 10].start()
+            (gate_in, down_in)[code // 100 % 10][code % 100].start()
         else:
             run[code // 100](code // 50 % 2, code % 50 // 10, code % 10)
     for t in range(steps):
@@ -475,7 +474,6 @@
     steps, rows, d_model = x_seq.shape
     ff = w_gate.shape[1]
     chips = tp // 2
-    n_sem = (2 * (ff // GATE_TILE) + d_model // DOWN_TILE) * FETCHES
     hid, _ = pl.pallas_call(
         functools.partial(mlp_kernel, chips),
         out_shape=(pltpu.VMEM((steps, rows, d_model), BF16), pltpu.VMEM(part.shape, BF16)),
@@ -495,7 +493,7 @@
             pltpu.VMEM((steps, SLOT_ROWS, d_model), BF16),
             pltpu.VMEM((steps, 2, SLOT_ROWS, d_model), BF16),
             pltpu.VMEM((rows, ff), BF16),
-            pltpu.SemaphoreType.DMA((n_sem,)),
+            pltpu.SemaphoreType.DMA((3, FETCHES)),
             pltpu.SemaphoreType.DMA((steps,)),
             pltpu.SemaphoreType.DMA((2, steps, len(COPIES))),
             pltpu.SemaphoreType.DMA((2, steps, len(COPIES))),

time: 103 us -> 100 us (0.971)
  Pallas kernels: 102 us -> 99.2 us
    pallas_call x1, Pallas kernels: 16.9 us -> 15.1 us  [run_qkv(): pl.pallas_call(functools.partial(qkv_kernel, tp, width * tp, hd * tp), ou...]
    pallas_call x1, Pallas kernels: 70.9 us -> 69.8 us  [run_mlp(): pl.pallas_call(functools.partial(mlp_kernel, chips), out_shape=(pltpu.VME...]
where the time goes in v7:
time: 100 us
  Pallas kernels  99.2 us (99%)
    pallas_call x1, Pallas kernels, run_mlp(): pl.pallas_call(functools.partial(mlp_kernel, chips), out_shape=(pltpu.VME...  69.8 us
    pallas_call x1, Pallas kernels, run_qkv(): pl.pallas_call(functools.partial(qkv_kernel, tp, width * tp, hd * tp), ou...  15.1 us
    pallas_call x1, Pallas kernels, run_attention(): pl.pallas_call(functools.partial(attention_kernel, steps, heads), out_sha...  12.6 us

profile of v7, /device:TPU:81, one launch (start us, length us, event | category | flops | bytes accessed | tf_op | source)
XLA Modules:
  0.0 100.1 jit_solution(244622642495301048)
XLA Ops:
  0.6 0.0 copy-start
  0.6 15.1 %qkv.1 = (bf16[128,16,128]{2,1,0:T(8,128)(2,1)S(1)}, f32[3,128,128]{2,1,0:T(8,128)S(1)}, f32[3,128,128]{2,1,0:T(8,128)S(1)}, bf16[128,256,128]{2,1,0:T(8,128)(2,1)S(1)}, bf16[128,256,128]{2,1,0:T(8,128)(2,1)S(1)}) custom-call(bf16[3,128,4096]{2,1,0:T(8,128)(2,1)} %x_hbm.3, s32[1,128]{1,0:T(1,128)} %bitcast.13, f32[1,128]{1,0:T(1,128)} %constant.2.clone.freq_hbm, ...), custom_call_target="tpu_custom_call" | custom-call | tf_op jit(solution)/shard_map/qkv/pallas_call | solution.py:144
  15.8 0.0 copy-done
  15.8 12.6 %attention.1 = (bf16[128,256,128]{2,1,0:T(8,128)(2,1)}, bf16[128,256,128]{2,1,0:T(8,128)(2,1)}, bf16[3,4,2,16,4096]{4,3,2,1,0:T(8,128)(2,1)S(1)}) custom-call(s32[128]{0:T(128)S(1)} %copy-done, bf16[128,16,128]{2,1,0:T(8,128)(2,1)S(1)} %get-tuple-element.12.q_ref, f32[3,128,128]{2,1,0:T(8,128)S(1)} %get-tuple-element.13.kn_ref, ...), custom_call_target="tpu_custom_call" | custom-call | tf_op jit(solution)/shard_map/attention/pallas_call | solution.py:259
  28.4 69.8 %mlp.1 = (bf16[3,128,4096]{2,1,0:T(8,128)(2,1)S(1)}, bf16[3,4,2,16,4096]{4,3,2,1,0:T(8,128)(2,1)S(1)}) custom-call(bf16[3,128,4096]{2,1,0:T(8,128)(2,1)} %x_hbm.3, bf16[3,4,2,16,4096]{4,3,2,1,0:T(8,128)(2,1)S(1)} %get-tuple-element.17.part_in, bf16[4096,1792]{1,0:T(8,128)(2,1)} %w1_hbm.1, ...), custom_call_target="tpu_custom_call", output_to_operand_aliasing={{1}: (1, {})} | custom-call | tf_op jit(solution)/shard_map/mlp/pallas_call | solution.py:477
  98.2 1.7 %store.1 = bf16[3,128,4096]{2,1,0:T(8,128)(2,1)} custom-call(bf16[3,128,4096]{2,1,0:T(8,128)(2,1)S(1)} %get-tuple-element.18.src), custom_call_target="tpu_custom_call" | custom-call | tf_op jit(solution)/shard_map/store/pallas_call | solution.py:517
Async XLA Ops:
  0.6 15.1 %copy-start = (s32[128]{0:T(128)S(1)}, s32[128]{0:T(128)}, u32[]{:S(2)}) copy-start(s32[128]{0:T(128)} %len_ref.1) | copy-start | bytes 1540

commit v8 on v7

--- a/solution.py
+++ b/solution.py
@@ -87,7 +87,8 @@
     for j in range(2):
         if j == 0:
             wq_in.wait()
-            cache_in[0].start()
+            for copy in cache_in[:CACHE_PARTS]:
+                copy.start()
         val = matmul(x_buf[...], wq_buf[:, j * half:(j + 1) * half]).astype(BF16).astype(F32)
         q_raw[:, j * half:(j + 1) * half] = val
         sq = jnp.sum(val * val, axis=1, keepdims=True)
@@ -106,7 +107,7 @@
             device_id={"tp": lax.rem(me + j, tp)}, device_id_type=MESH)
         copy.start()
         copies.append(copy)
-    for copy in cache_in[1:]:
+    for copy in cache_in[CACHE_PARTS:]:
         copy.start()
     total = part[...]
     for j in range(1, tp):

time: 100 us -> 99.7 us (level)
  no operation moved by 1% of the time
where the time goes in v8:
time: 99.7 us; the launch traced here: 99.6 us
  Pallas kernels  98.7 us (99%)
    pallas_call x1, Pallas kernels, run_mlp(): pl.pallas_call(functools.partial(mlp_kernel, chips), out_shape=(pltpu.VME...  69.3 us
    pallas_call x1, Pallas kernels, run_qkv(): pl.pallas_call(functools.partial(qkv_kernel, tp, width * tp, hd * tp), ou...  15.1 us
    pallas_call x1, Pallas kernels, run_attention(): pl.pallas_call(functools.partial(attention_kernel, steps, heads), out_sha...  12.6 us

profile of v8, /device:TPU:81, one launch (start us, length us, event | category | flops | bytes accessed | tf_op | source)
XLA Modules:
  0.0 99.6 jit_solution(17002758126021511266)
XLA Ops:
  0.6 0.0 copy-start
  0.6 15.1 %qkv.1 = (bf16[128,16,128]{2,1,0:T(8,128)(2,1)S(1)}, f32[3,128,128]{2,1,0:T(8,128)S(1)}, f32[3,128,128]{2,1,0:T(8,128)S(1)}, bf16[128,256,128]{2,1,0:T(8,128)(2,1)S(1)}, bf16[128,256,128]{2,1,0:T(8,128)(2,1)S(1)}) custom-call(bf16[3,128,4096]{2,1,0:T(8,128)(2,1)} %x_hbm.3, s32[1,128]{1,0:T(1,128)} %bitcast.13, f32[1,128]{1,0:T(1,128)} %constant.2.clone.freq_hbm, ...), custom_call_target="tpu_custom_call" | custom-call | tf_op jit(solution)/shard_map/qkv/pallas_call | solution.py:145
  15.8 0.0 copy-done
  15.8 12.6 %attention.1 = (bf16[128,256,128]{2,1,0:T(8,128)(2,1)}, bf16[128,256,128]{2,1,0:T(8,128)(2,1)}, bf16[3,4,2,16,4096]{4,3,2,1,0:T(8,128)(2,1)S(1)}) custom-call(s32[128]{0:T(128)S(1)} %copy-done, bf16[128,16,128]{2,1,0:T(8,128)(2,1)S(1)} %get-tuple-element.12.q_ref, f32[3,128,128]{2,1,0:T(8,128)S(1)} %get-tuple-element.13.kn_ref, ...), custom_call_target="tpu_custom_call" | custom-call | tf_op jit(solution)/shard_map/attention/pallas_call | solution.py:260
  28.4 69.3 %mlp.1 = (bf16[3,128,4096]{2,1,0:T(8,128)(2,1)S(1)}, bf16[3,4,2,16,4096]{4,3,2,1,0:T(8,128)(2,1)S(1)}) custom-call(bf16[3,128,4096]{2,1,0:T(8,128)(2,1)} %x_hbm.3, bf16[3,4,2,16,4096]{4,3,2,1,0:T(8,128)(2,1)S(1)} %get-tuple-element.17.part_in, bf16[4096,1792]{1,0:T(8,128)(2,1)} %w1_hbm.1, ...), custom_call_target="tpu_custom_call", output_to_operand_aliasing={{1}: (1, {})} | custom-call | tf_op jit(solution)/shard_map/mlp/pallas_call | solution.py:478
  97.7 1.7 %store.1 = bf16[3,128,4096]{2,1,0:T(8,128)(2,1)} custom-call(bf16[3,128,4096]{2,1,0:T(8,128)(2,1)S(1)} %get-tuple-element.18.src), custom_call_target="tpu_custom_call" | custom-call | tf_op jit(solution)/shard_map/store/pallas_call | solution.py:518
Async XLA Ops:
  0.6 15.1 %copy-start = (s32[128]{0:T(128)S(1)}, s32[128]{0:T(128)}, u32[]{:S(2)}) copy-start(s32[128]{0:T(128)} %len_ref.1) | copy-start | bytes 1540
